TPU v7x, 256 devices: a whole 4x4x8 slice. The times are simulated.
256 devices in a mesh: blk: 128 (over z, x, y), rep: 2 (over core).
Axes of the slice: x: 4, y: 4, z: 8, core: 2. Of those that a mesh axis runs over, the one named last changes fastest.
Arguments:
- points: float32 [128, 3, 8192], P('blk'), may hold values from -6 to 6
- normals: float32 [128, 3, 8192], P('blk'), may hold values from -6 to 6
- src_block: int32 [8, 128, 1, 16], P(None, 'blk', None, 'rep'), may hold values from 0 to 63
- tgt_index: int32 [8, 128, 1, 16, 128], P(None, 'blk', None, 'rep'), may hold values from 0 to 8191
- active: int32 [8, 128, 1], P(None, 'blk'), may hold values from 0 to 16
Outputs:
- diag_hess: float32 [128, 36], P('blk')
- gradient: float32 [128, 6], P('blk')
- pair_hess: float32 [8, 128, 1, 36], P(None, 'blk')
Inputs may be any that keep to these rules, and one draw needn't show every extreme that they name: Slots j with j >= active contribute nothing.
All inputs are finite; a program needn't handle non-finite values.
Results may differ from a plain program's by a relative error of at most 0.00017.
Values sent between devices are 32-bit elements; how exact they have to be, the bound alone decides.
No kernel may reach another device: no remote copies, remote signals or barrier semaphores. Data moves between devices by JAX's collectives and lax.ppermute only.
A program may use at most 64 MiB of HBM per device.

v0:
```python
import functools

import jax
import jax.numpy as jnp
from jax import lax
from jax.experimental import pallas as pl
from jax.experimental.pallas import tpu as pltpu
from jax.sharding import PartitionSpec as P


NB = 16
BLOCK = 128
LANES = 128
SUBLANES = 8
FAR = 4


VMEM = pl.BlockSpec(memory_space=pltpu.VMEM)
SMEM = pl.BlockSpec(memory_space=pltpu.SMEM)


def routed(block, blk, shifts):
    route = [(i * 2 + r, (i + shifts[r]) % blk * 2 + r) for i in range(blk) for r in range(2)]
    return lax.ppermute(block, ("blk", "rep"), route)


def swapped(block):
    return lax.ppermute(block, "rep", [(0, 1), (1, 0)])


def near(x):
    return pltpu.with_memory_space_constraint(x, pltpu.VMEM)


def pick_lanes(row, lanes):
    return lax.gather(
        row,
        lanes[:, :, None],
        lax.GatherDimensionNumbers(
            offset_dims=(),
            collapsed_slice_dims=(1,),
            start_index_map=(1,),
            operand_batching_dims=(0,),
            start_indices_batching_dims=(0,),
        ),
        slice_sizes=(1, 1),
        mode=lax.GatherScatterMode.PROMISE_IN_BOUNDS,
    )


def step_of(m, rep):
    return rep if m else 3 - rep


def pack_kernel(src_ref, active_ref, points_ref, normals_ref, index_ref, table_ref, *outs):
    half = lax.axis_index("rep")
    slot = lax.broadcasted_iota(jnp.int32, (SUBLANES, LANES), 0) + half * SUBLANES
    for other, out in enumerate(outs):
        for m in range(2):
            for far in range(2):
                k = step_of(m, 1 - half if other else half) + FAR * far
                for j in range(SUBLANES):
                    b = src_ref[k, j]
                    for c in range(3):
                        out[m, far, c, pl.ds(j, 1), :] = points_ref[c, pl.ds(b, 1), :]
                live = slot < active_ref[0, k]
                out[m, far, 3] = jnp.where(live, index_ref[k], -1).astype(jnp.float32)
    table_ref[0:3] = points_ref[...]
    table_ref[3:6] = normals_ref[...]


def merge_kernel(own_ref, other_ref, *outs):
    for m, out in enumerate(outs):
        for far in range(2):
            for c in range(4):
                out[far, c, pl.ds(0, SUBLANES), :] = own_ref[m, far, c]
                out[far, c, pl.ds(SUBLANES, SUBLANES), :] = other_ref[m, far, c]


def pair_kernel(table_ref, message_ref, *refs, far):
    rows_ref, totals_ref, sums_s = refs[-3:]
    shape = (SUBLANES, LANES)
    index = [message_ref[far, 3, pl.ds(h * SUBLANES, SUBLANES), :].astype(jnp.int32) for h in range(2)]
    lanes = [i & (LANES - 1) for i in index]
    high = [i >> 7 for i in index]
    found = [[jnp.zeros(shape, jnp.float32) for _ in range(6)] for _ in range(2)]
    for r in range(table_ref.shape[1]):
        here = [h == r for h in high]
        for c in range(6):
            line = jnp.broadcast_to(table_ref[c, pl.ds(r, 1), :], shape)
            for h in range(2):
                found[h][c] = jnp.where(here[h], pick_lanes(line, lanes[h]), found[h][c])
    parts = []
    for h in range(2):
        p = [message_ref[far, c, pl.ds(h * SUBLANES, SUBLANES), :] for c in range(3)]
        q, n = found[h][:3], found[h][3:]
        resid = n[0] * (p[0] - q[0]) + n[1] * (p[1] - q[1]) + n[2] * (p[2] - q[2])
        weight = 1.0 / (1.0 + resid * resid)
        jacob = [
            p[1] * n[2] - p[2] * n[1],
            p[2] * n[0] - p[0] * n[2],
            p[0] * n[1] - p[1] * n[0],
            n[0],
            n[1],
            n[2],
        ]
        scaled = [weight * x for x in jacob]
        terms = [scaled[a] * jacob[b] for a in range(6) for b in range(a, 6)]
        terms += [scaled[a] * resid for a in range(6)]
        parts.append(terms)
    for t in range(27):
        sums_s[pl.ds(t, 1), :] = jnp.sum(parts[0][t] + parts[1][t], axis=0, keepdims=True)

    row = lax.broadcasted_iota(jnp.int32, shape, 0)
    lane = lax.broadcasted_iota(jnp.int32, shape, 1)
    first, second = lane // 6, lane % 6
    low, top = jnp.minimum(first, second), jnp.maximum(first, second)
    gram_term = jnp.where(lane < 36, low * (11 - low) // 2 + top, -1)
    push_term = jnp.where(lane < 6, 21 + lane, -1)
    gram = jnp.zeros(shape, jnp.float32)
    push = jnp.zeros(shape, jnp.float32)
    for g in range(4):
        column = jnp.sum(sums_s[pl.ds(SUBLANES * g, SUBLANES), :], axis=1, keepdims=True)
        term = SUBLANES * g + row
        if g < 3:
            gram = jnp.where(gram_term == term, column, gram)
        if g > 1:
            push = jnp.where(push_term == term, column, push)
    scale = 1.0 / (NB * BLOCK)
    gram = jnp.sum(gram, axis=0, keepdims=True) * scale
    push = jnp.sum(push, axis=0, keepdims=True) * scale
    at = 2 * far
    if far:
        rows_ref[0:2, :] = refs[1][...]
    rows_ref[at : at + 1, :] = gram
    rows_ref[at + 1 : at + 2, :] = push
    totals_ref[...] = refs[0][...] if len(refs) > 3 else jnp.zeros((4, LANES), jnp.float32)
    totals_ref[at : at + 1, :] += gram
    totals_ref[at + 1 : at + 2, :] -= push


def join_kernel(own_ref, other_ref, here_ref, far_ref):
    here_ref[...] = own_ref[0:2, :] + other_ref[0:2, :]
    far_ref[...] = own_ref[2:4, :] + other_ref[2:4, :]


def finish_kernel(*refs, scale):
    rows, totals, (diag_ref, grad_ref, pair_ref) = refs[:4], refs[4:6], refs[6:]
    half = lax.axis_index("rep")
    total = totals[0][...] + totals[1][...]
    for i in range(4):
        m, other = i % 2, i // 2
        for far in range(2):
            k = step_of(m, 1 - half if other else half) + FAR * far
            got = rows[i][2 * far : 2 * far + 2, :]
            pair_ref[pl.ds(k, 1), :] = got[0:1, :36]
            total = total + got
    diag_ref[...] = total[0:1, :36] * scale
    grad_ref[...] = total[1:2, :6] * scale


def body(points, normals, src_block, tgt_index, active, *, blk):
    rounds = src_block.shape[0]
    scan = (3, points.shape[2] // LANES, LANES)
    f32 = jnp.float32
    steps = [tuple(step_of(m, rep) + 1 for rep in range(2)) for m in range(2)]
    table, own, other = pl.pallas_call(
        pack_kernel,
        in_specs=[SMEM, SMEM, VMEM, VMEM, VMEM],
        out_specs=[VMEM] * 3,
        out_shape=[pltpu.VMEM((6, *scan[1:]), f32)] + [pltpu.VMEM((2, 2, 4, SUBLANES, LANES), f32)] * 2,
        name="pack",
    )(
        src_block.reshape(rounds, SUBLANES),
        active.reshape(1, rounds),
        points.reshape(scan),
        normals.reshape(scan),
        tgt_index.reshape(rounds, SUBLANES, BLOCK),
    )
    other = swapped(other)
    far_table = routed(table, blk, (FAR, FAR))
    messages = pl.pallas_call(
        merge_kernel,
        in_specs=[VMEM] * 2,
        out_specs=[VMEM] * 2,
        out_shape=[pltpu.VMEM((2, 4, NB, LANES), f32)] * 2,
        name="merge",
    )(near(own), near(other))
    there = [routed(x, blk, tuple(-s for s in step)) for x, step in zip(messages, steps)]
    back, totals = [], []
    for message, step in zip(there, steps):
        rows = []
        for far in range(2):
            args = [far_table if far else table, message, *totals, *rows]
            *rows, last = pl.pallas_call(
                functools.partial(pair_kernel, far=far),
                in_specs=[VMEM] * len(args),
                out_specs=[VMEM] * 2,
                out_shape=[pltpu.VMEM((2 + 2 * far, LANES), f32), pltpu.VMEM((4, LANES), f32)],
                scratch_shapes=[pltpu.VMEM((32, LANES), f32)],
                name="pair",
            )(*map(near, args))
            totals = [last]
        back.append(routed(rows[0], blk, step))
    other_total = swapped(totals[0])
    here_total, far_total = pl.pallas_call(
        join_kernel,
        in_specs=[VMEM] * 2,
        out_specs=[VMEM] * 2,
        out_shape=[pltpu.VMEM((2, LANES), f32)] * 2,
        name="join",
    )(near(totals[0]), near(other_total))
    far_total = routed(far_total, blk, (-FAR, -FAR))
    others = []
    for x in back:
        others.append(swapped(x))
    diag, grad, pairs = pl.pallas_call(
        functools.partial(finish_kernel, scale=1.0 / (2.0 * rounds)),
        in_specs=[VMEM] * 6,
        out_specs=[VMEM] * 3,
        out_shape=[
            jax.ShapeDtypeStruct((1, 36), f32),
            jax.ShapeDtypeStruct((1, 6), f32),
            jax.ShapeDtypeStruct((rounds, 36), f32),
        ],
        name="finish",
    )(*(near(x) for x in (*back, *others, here_total, far_total)))
    return diag, grad, pairs.reshape(rounds, 1, 1, 36)


def solution(mesh):
    return jax.shard_map(
        functools.partial(body, blk=mesh.shape["blk"]),
        mesh=mesh,
        in_specs=(
            P("blk", None, None),
            P("blk", None, None),
            P(None, "blk", None, "rep"),
            P(None, "blk", None, "rep", None),
            P(None, "blk", None),
        ),
        out_specs=(P("blk", None), P("blk", None), P(None, "blk", None, None)),
        check_vma=False,
    )
```

profile of v0, /device:TPU:1, one launch (start us, length us, event | category | flops | bytes accessed | tf_op | source)
XLA Modules:
  0.0 34.2 jit_solution(3310572827890466963)
XLA Ops:
  0.6 1.1 %pack.1 = (f32[6,64,128]{2,1,0:T(8,128)S(1)}, f32[2,2,4,8,128]{4,3,2,1,0:T(8,128)S(1)}, f32[2,2,4,8,128]{4,3,2,1,0:T(8,128)S(1)}) custom-call(s32[8,8]{1,0:T(8,128)} %bitcast.11, s32[1,8]{1,0:T(1,128)} %bitcast.12, f32[3,64,128]{2,1,0:T(8,128)} %bitcast.8, f32[3,64,128]{2,1,0:T(8,128)} %bitcast.9, s32[8,8,128]{2,1,0:T(8,128)} %bitcast.10), custom_call_target="tpu_custom_call" | custom-call | tf_op jit(solution)/shard_map/pack/pallas_call | solution.py:167
  1.7 2.1 %collective-permute-start = (f32[6,64,128]{2,1,0:T(8,128)S(1)}, f32[6,64,128]{2,1,0:T(8,128)S(1)}, u32[]{:S(2)}, u32[]{:S(2)}) collective-permute-start(f32[6,64,128]{2,1,0:T(8,128)S(1)} %get-tuple-element.21.table_ref), channel_id=1, source_target_pairs={{0,8},{1,9},{2,10},{3,11},{4,12},{5,13},{6,14},{7,15},{8,16},{9,17... | collective-permute-start | bytes 589832 | tf_op jit(solution)/shard_map/ppermute | solution.py:24
  3.8 1.3 %collective-permute-start.1 = (f32[2,2,4,8,128]{4,3,2,1,0:T(8,128)S(1)}, f32[2,2,4,8,128]{4,3,2,1,0:T(8,128)S(1)}, u32[]{:S(2)}, u32[]{:S(2)}) collective-permute-start(f32[2,2,4,8,128]{4,3,2,1,0:T(8,128)S(1)} %get-tuple-element.23), channel_id=1, source_target_pairs={{0,1},{1,0},{2,3},{3,2},{4,5},{5,4},{6,7},{7,6},{8,9},{9,8},{10,11... | collective-permute-start | bytes 196616 | tf_op jit(solution)/shard_map/ppermute | solution.py:28
  5.1 0.9 %collective-permute-done.1.other_ref = f32[2,2,4,8,128]{4,3,2,1,0:T(8,128)S(1)} collective-permute-done((f32[2,2,4,8,128]{4,3,2,1,0:T(8,128)S(1)}, f32[2,2,4,8,128]{4,3,2,1,0:T(8,128)S(1)}, u32[]{:S(2)}, u32[]{:S(2)}) %collective-permute-start.1) | collective-permute-done | bytes 65568 | tf_op jit(solution)/shard_map/ppermute | solution.py:28
  6.0 7.1 %collective-permute-start.2 = (f32[2,4,16,128]{3,2,1,0:T(8,128)S(1)}, f32[2,4,16,128]{3,2,1,0:T(8,128)S(1)}, u32[]{:S(2)}, u32[]{:S(2)}) collective-permute-start(f32[2,4,16,128]{3,2,1,0:T(8,128)S(1)} %get-tuple-element.24), channel_id=1, source_target_pairs={{0,248},{1,251},{2,250},{3,253},{4,252},{5,255},{6,254},{7,1},{8,0... | collective-permute-start | bytes 196616 | tf_op jit(solution)/shard_map/ppermute | solution.py:24
  13.2 4.0 %collective-permute-start.4 = (f32[2,4,16,128]{3,2,1,0:T(8,128)S(1)}, f32[2,4,16,128]{3,2,1,0:T(8,128)S(1)}, u32[]{:S(2)}, u32[]{:S(2)}) collective-permute-start(f32[2,4,16,128]{3,2,1,0:T(8,128)S(1)} %get-tuple-element.28), channel_id=1, source_target_pairs={{0,254},{1,253},{2,0},{3,255},{4,2},{5,1},{6,4},{7,3},{8,6},{9,5},... | collective-permute-start | bytes 196616 | tf_op jit(solution)/shard_map/ppermute | solution.py:24
  17.1 0.0 collective-permute-done.2.message_ref
  17.1 1.0 %pair.4 = (f32[2,128]{1,0:T(2,128)S(1)}, f32[4,128]{1,0:T(4,128)S(1)}) custom-call(f32[6,64,128]{2,1,0:T(8,128)S(1)} %get-tuple-element.21.table_ref, f32[2,4,16,128]{3,2,1,0:T(8,128)S(1)} %collective-permute-done.2.message_ref), custom_call_target="tpu_custom_call" | custom-call | tf_op jit(solution)/shard_map/pair/pallas_call | solution.py:195
  18.2 0.0 collective-permute-done.table_ref
  18.2 1.0 %pair.5 = (f32[4,128]{1,0:T(4,128)S(1)}, f32[4,128]{1,0:T(4,128)S(1)}) custom-call(f32[6,64,128]{2,1,0:T(8,128)S(1)} %collective-permute-done.table_ref, f32[2,4,16,128]{3,2,1,0:T(8,128)S(1)} %collective-permute-done.2.message_ref, f32[4,128]{1,0:T(4,128)S(1)} %get-tuple-element.25.refs_0_, f32[2,128]{1,0:T(2,128)S(1)} %get-tuple-element.26.refs_1_), custom_call_target="tpu_custom_call" | custom-call | tf_op jit(solution)/shard_map/pair/pallas_call | solution.py:195
  19.3 0.0 collective-permute-done.4.message_ref
  19.3 1.0 %pair.6 = (f32[2,128]{1,0:T(2,128)S(1)}, f32[4,128]{1,0:T(4,128)S(1)}) custom-call(f32[6,64,128]{2,1,0:T(8,128)S(1)} %get-tuple-element.21.table_ref, f32[2,4,16,128]{3,2,1,0:T(8,128)S(1)} %collective-permute-done.4.message_ref, f32[4,128]{1,0:T(4,128)S(1)} %get-tuple-element.29.refs_0_), custom_call_target="tpu_custom_call" | custom-call | tf_op jit(solution)/shard_map/pair/pallas_call | solution.py:195
  20.3 1.0 %pair.7 = (f32[4,128]{1,0:T(4,128)S(1)}, f32[4,128]{1,0:T(4,128)S(1)}) custom-call(f32[6,64,128]{2,1,0:T(8,128)S(1)} %collective-permute-done.table_ref, f32[2,4,16,128]{3,2,1,0:T(8,128)S(1)} %collective-permute-done.4.message_ref, f32[4,128]{1,0:T(4,128)S(1)} %get-tuple-element.30.refs_0_, f32[2,128]{1,0:T(2,128)S(1)} %get-tuple-element.31.refs_1_), custom_call_target="tpu_custom_call" | custom-call | tf_op jit(solution)/shard_map/pair/pallas_call | solution.py:195
  21.4 2.6 %collective-permute-start.5 = (f32[4,128]{1,0:T(4,128)S(1)}, f32[4,128]{1,0:T(4,128)S(1)}, u32[]{:S(2)}, u32[]{:S(2)}) collective-permute-start(f32[4,128]{1,0:T(4,128)S(1)} %get-tuple-element.32), channel_id=1, source_target_pairs={{0,2},{1,5},{2,4},{3,7},{4,6},{5,9},{6,8},{7,11},{8,10},{9,13},{10... | collective-permute-start | bytes 6152 | tf_op jit(solution)/shard_map/ppermute | solution.py:24
  24.0 0.0 collective-permute-start.3
  24.0 0.0 collective-permute-start.8
  24.0 5.7 %collective-permute-done.5.refs_1_ = f32[4,128]{1,0:T(4,128)S(1)} collective-permute-done((f32[4,128]{1,0:T(4,128)S(1)}, f32[4,128]{1,0:T(4,128)S(1)}, u32[]{:S(2)}, u32[]{:S(2)}) %collective-permute-start.5) | collective-permute-done | bytes 2080 | tf_op jit(solution)/shard_map/ppermute | solution.py:24
  29.6 1.5 %collective-permute-start.7 = (f32[4,128]{1,0:T(4,128)S(1)}, f32[4,128]{1,0:T(4,128)S(1)}, u32[]{:S(2)}, u32[]{:S(2)}) collective-permute-start(f32[4,128]{1,0:T(4,128)S(1)} %collective-permute-done.5.refs_1_), channel_id=1, source_target_pairs={{0,1},{1,0},{2,3},{3,2},{4,5},{5,4},{6,7},{7,6},{8,9},{9,8},{10,11... | collective-permute-start | bytes 6152 | tf_op jit(solution)/shard_map/ppermute | solution.py:28
  31.1 0.0 collective-permute-done.3.refs_0_
  31.1 0.0 collective-permute-start.6
  31.1 0.0 collective-permute-done.8.other_ref
  31.1 1.2 %collective-permute-start.9 = (f32[2,128]{1,0:T(2,128)S(1)}, f32[2,128]{1,0:T(2,128)S(1)}, u32[]{:S(2)}, u32[]{:S(2)}) collective-permute-start(f32[2,128]{1,0:T(2,128)S(1)} %get-tuple-element.35), channel_id=1, source_target_pairs={{0,248},{1,249},{2,250},{3,251},{4,252},{5,253},{6,254},{7,255},{8... | collective-permute-start | bytes 3080 | tf_op jit(solution)/shard_map/ppermute | solution.py:24
  32.4 1.3 %collective-permute-done.9.refs_5_ = f32[2,128]{1,0:T(2,128)S(1)} collective-permute-done((f32[2,128]{1,0:T(2,128)S(1)}, f32[2,128]{1,0:T(2,128)S(1)}, u32[]{:S(2)}, u32[]{:S(2)}) %collective-permute-start.9) | collective-permute-done | bytes 1056 | tf_op jit(solution)/shard_map/ppermute | solution.py:24
  33.6 0.0 collective-permute-done.7.refs_3_
  33.6 0.0 collective-permute-done.6.refs_2_
  33.6 0.6 %finish.1 = (f32[1,36]{1,0:T(1,128)}, f32[1,6]{1,0:T(1,128)}, f32[8,36]{1,0:T(8,128)}) custom-call(f32[4,128]{1,0:T(4,128)S(1)} %collective-permute-done.3.refs_0_, f32[4,128]{1,0:T(4,128)S(1)} %collective-permute-done.5.refs_1_, f32[4,128]{1,0:T(4,128)S(1)} %collective-permute-done.6.refs_2_, f32[4,128]{1,0:T(4,128)S(1)} %collective-permute-done.7.refs_3_, ...), custom_call_target="tpu_custom_call" | custom-call | tf_op jit(solution)/shard_map/finish/pallas_call | solution.py:217
  (2 shorter events, 0.0 us)
Async XLA Ops:
  1.7 16.5 %collective-permute-start = (f32[6,64,128]{2,1,0:T(8,128)S(1)}, f32[6,64,128]{2,1,0:T(8,128)S(1)}, u32[]{:S(2)}, u32[]{:S(2)}) collective-permute-start(f32[6,64,128]{2,1,0:T(8,128)S(1)} %get-tuple-element.21.table_ref), channel_id=1, source_target_pairs={{0,8},{1,9},{2,10},{3,11},{4,12},{5,13},{6,14},{7,15},{8,16},{9,17... | collective-permute-start | bytes 589832 | tf_op jit(solution)/shard_map/ppermute | solution.py:24
  3.8 2.2 %collective-permute-start.1 = (f32[2,2,4,8,128]{4,3,2,1,0:T(8,128)S(1)}, f32[2,2,4,8,128]{4,3,2,1,0:T(8,128)S(1)}, u32[]{:S(2)}, u32[]{:S(2)}) collective-permute-start(f32[2,2,4,8,128]{4,3,2,1,0:T(8,128)S(1)} %get-tuple-element.23), channel_id=1, source_target_pairs={{0,1},{1,0},{2,3},{3,2},{4,5},{5,4},{6,7},{7,6},{8,9},{9,8},{10,11... | collective-permute-start | bytes 196616 | tf_op jit(solution)/shard_map/ppermute | solution.py:28
  6.0 11.1 %collective-permute-start.2 = (f32[2,4,16,128]{3,2,1,0:T(8,128)S(1)}, f32[2,4,16,128]{3,2,1,0:T(8,128)S(1)}, u32[]{:S(2)}, u32[]{:S(2)}) collective-permute-start(f32[2,4,16,128]{3,2,1,0:T(8,128)S(1)} %get-tuple-element.24), channel_id=1, source_target_pairs={{0,248},{1,251},{2,250},{3,253},{4,252},{5,255},{6,254},{7,1},{8,0... | collective-permute-start | bytes 196616 | tf_op jit(solution)/shard_map/ppermute | solution.py:24
  13.2 6.1 %collective-permute-start.4 = (f32[2,4,16,128]{3,2,1,0:T(8,128)S(1)}, f32[2,4,16,128]{3,2,1,0:T(8,128)S(1)}, u32[]{:S(2)}, u32[]{:S(2)}) collective-permute-start(f32[2,4,16,128]{3,2,1,0:T(8,128)S(1)} %get-tuple-element.28), channel_id=1, source_target_pairs={{0,254},{1,253},{2,0},{3,255},{4,2},{5,1},{6,4},{7,3},{8,6},{9,5},... | collective-permute-start | bytes 196616 | tf_op jit(solution)/shard_map/ppermute | solution.py:24
  21.4 8.3 %collective-permute-start.5 = (f32[4,128]{1,0:T(4,128)S(1)}, f32[4,128]{1,0:T(4,128)S(1)}, u32[]{:S(2)}, u32[]{:S(2)}) collective-permute-start(f32[4,128]{1,0:T(4,128)S(1)} %get-tuple-element.32), channel_id=1, source_target_pairs={{0,2},{1,5},{2,4},{3,7},{4,6},{5,9},{6,8},{7,11},{8,10},{9,13},{10... | collective-permute-start | bytes 6152 | tf_op jit(solution)/shard_map/ppermute | solution.py:24
  24.0 7.1 %collective-permute-start.3 = (f32[4,128]{1,0:T(4,128)S(1)}, f32[4,128]{1,0:T(4,128)S(1)}, u32[]{:S(2)}, u32[]{:S(2)}) collective-permute-start(f32[4,128]{1,0:T(4,128)S(1)} %get-tuple-element.27), channel_id=1, source_target_pairs={{0,8},{1,7},{2,10},{3,9},{4,12},{5,11},{6,14},{7,13},{8,16},{9,15}... | collective-permute-start | bytes 6152 | tf_op jit(solution)/shard_map/ppermute | solution.py:24
  24.0 7.1 %collective-permute-start.8 = (f32[4,128]{1,0:T(4,128)S(1)}, f32[4,128]{1,0:T(4,128)S(1)}, u32[]{:S(2)}, u32[]{:S(2)}) collective-permute-start(f32[4,128]{1,0:T(4,128)S(1)} %get-tuple-element.33.own_ref), channel_id=1, source_target_pairs={{0,1},{1,0},{2,3},{3,2},{4,5},{5,4},{6,7},{7,6},{8,9},{9,8},{10,11... | collective-permute-start | bytes 6152 | tf_op jit(solution)/shard_map/ppermute | solution.py:28
  29.6 4.0 %collective-permute-start.7 = (f32[4,128]{1,0:T(4,128)S(1)}, f32[4,128]{1,0:T(4,128)S(1)}, u32[]{:S(2)}, u32[]{:S(2)}) collective-permute-start(f32[4,128]{1,0:T(4,128)S(1)} %collective-permute-done.5.refs_1_), channel_id=1, source_target_pairs={{0,1},{1,0},{2,3},{3,2},{4,5},{5,4},{6,7},{7,6},{8,9},{9,8},{10,11... | collective-permute-start | bytes 6152 | tf_op jit(solution)/shard_map/ppermute | solution.py:28
  31.1 2.5 %collective-permute-start.6 = (f32[4,128]{1,0:T(4,128)S(1)}, f32[4,128]{1,0:T(4,128)S(1)}, u32[]{:S(2)}, u32[]{:S(2)}) collective-permute-start(f32[4,128]{1,0:T(4,128)S(1)} %collective-permute-done.3.refs_0_), channel_id=1, source_target_pairs={{0,1},{1,0},{2,3},{3,2},{4,5},{5,4},{6,7},{7,6},{8,9},{9,8},{10,11... | collective-permute-start | bytes 6152 | tf_op jit(solution)/shard_map/ppermute | solution.py:28
  31.1 2.5 %collective-permute-start.9 = (f32[2,128]{1,0:T(2,128)S(1)}, f32[2,128]{1,0:T(2,128)S(1)}, u32[]{:S(2)}, u32[]{:S(2)}) collective-permute-start(f32[2,128]{1,0:T(2,128)S(1)} %get-tuple-element.35), channel_id=1, source_target_pairs={{0,248},{1,249},{2,250},{3,251},{4,252},{5,253},{6,254},{7,255},{8... | collective-permute-start | bytes 3080 | tf_op jit(solution)/shard_map/ppermute | solution.py:24
where the time goes:
time: 34.4 us; the launch traced here: 34.2 us
  starting transfers between devices  19.8 us (58%)
  waiting for transfers between devices  7.83 us (23%)
  Pallas kernels  5.88 us (17%)
  between operations  0.7 us (2%)
    ppermute x6, starting transfers between devices, routed(): return lax.ppermute(block, ('blk', 'rep'), route)  17.1 us
    ppermute x6, waiting for transfers between devices, routed(): return lax.ppermute(block, ('blk', 'rep'), route)  6.92 us
    pallas_call x4, Pallas kernels, body(): pl.pallas_call(functools.partial(pair_kernel, far=far), in_specs=[VMEM] *...  4.17 us
    ppermute x4, starting transfers between devices, swapped(): return lax.ppermute(block, 'rep', [(0, 1), (1, 0)])  2.74 us
    pallas_call x1, Pallas kernels, body(): pl.pallas_call(pack_kernel, in_specs=[SMEM, SMEM, VMEM, VMEM, VMEM], out_...  1.08 us
    ppermute x4, waiting for transfers between devices, swapped(): return lax.ppermute(block, 'rep', [(0, 1), (1, 0)])  0.91 us
  transfers between devices with their start and end apart: 10, of which 3 were waited for; matrix products, arithmetic and copies ran while one was open for 0% of the time, Pallas kernels for 6%

commit v1 on v0

--- a/solution.py
+++ b/solution.py
@@ -139,9 +139,13 @@
     totals_ref[at + 1 : at + 2, :] -= push
 
 
-def join_kernel(own_ref, other_ref, here_ref, far_ref):
-    here_ref[...] = own_ref[0:2, :] + other_ref[0:2, :]
-    far_ref[...] = own_ref[2:4, :] + other_ref[2:4, :]
+def split_kernel(totals_ref, here_ref, far_ref):
+    here_ref[...] = totals_ref[0:2, :]
+    far_ref[...] = totals_ref[2:4, :]
+
+
+def join_kernel(here_ref, far_ref, total_ref):
+    total_ref[...] = here_ref[...] + far_ref[...]
 
 
 def finish_kernel(*refs, scale):
@@ -202,15 +206,15 @@
             )(*map(near, args))
             totals = [last]
         back.append(routed(rows[0], blk, step))
-    other_total = swapped(totals[0])
+    total = pltpu.VMEM((2, LANES), f32)
     here_total, far_total = pl.pallas_call(
-        join_kernel,
-        in_specs=[VMEM] * 2,
-        out_specs=[VMEM] * 2,
-        out_shape=[pltpu.VMEM((2, LANES), f32)] * 2,
-        name="join",
-    )(near(totals[0]), near(other_total))
+        split_kernel, in_specs=[VMEM], out_specs=[VMEM] * 2, out_shape=[total] * 2, name="split"
+    )(near(totals[0]))
     far_total = routed(far_total, blk, (-FAR, -FAR))
+    total = pl.pallas_call(
+        join_kernel, in_specs=[VMEM] * 2, out_specs=VMEM, out_shape=total, name="join"
+    )(near(here_total), near(far_total))
+    other_total = swapped(total)
     others = []
     for x in back:
         others.append(swapped(x))
@@ -224,7 +228,7 @@
             jax.ShapeDtypeStruct((rounds, 36), f32),
         ],
         name="finish",
-    )(*(near(x) for x in (*back, *others, here_total, far_total)))
+    )(*(near(x) for x in (*back, *others, total, other_total)))
     return diag, grad, pairs.reshape(rounds, 1, 1, 36)
 
 

time: 34.4 us -> 33.2 us (0.965)
  waiting for transfers between devices: 7.83 us -> 2.43 us
  starting transfers between devices: 19.8 us -> 24.1 us
    ppermute x6, waiting for transfers between devices: 6.92 us -> 0.7 us  [routed(): return lax.ppermute(block, ('blk', 'rep'), route)]
    ppermute x6, starting transfers between devices: 17.1 us -> 20.8 us  [routed(): return lax.ppermute(block, ('blk', 'rep'), route)]
    ppermute x4, waiting for transfers between devices: 0.91 us -> 1.73 us  [swapped(): return lax.ppermute(block, 'rep', [(0, 1), (1, 0)])]
    ppermute x4, starting transfers between devices: 2.74 us -> 3.24 us  [swapped(): return lax.ppermute(block, 'rep', [(0, 1), (1, 0)])]
where the time goes in v1:
time: 33.2 us; the launch traced here: 33.1 us
  starting transfers between devices  24.1 us (73%)
  Pallas kernels  5.88 us (18%)
  waiting for transfers between devices  2.43 us (7%)
  between operations  0.7 us (2%)
    ppermute x6, starting transfers between devices, routed(): return lax.ppermute(block, ('blk', 'rep'), route)  20.8 us
    pallas_call x4, Pallas kernels, body(): pl.pallas_call(functools.partial(pair_kernel, far=far), in_specs=[VMEM] *...  4.17 us
    ppermute x4, starting transfers between devices, swapped(): return lax.ppermute(block, 'rep', [(0, 1), (1, 0)])  3.24 us
    ppermute x4, waiting for transfers between devices, swapped(): return lax.ppermute(block, 'rep', [(0, 1), (1, 0)])  1.73 us
    pallas_call x1, Pallas kernels, body(): pl.pallas_call(pack_kernel, in_specs=[SMEM, SMEM, VMEM, VMEM, VMEM], out_...  1.08 us
    ppermute x6, waiting for transfers between devices, routed(): return lax.ppermute(block, ('blk', 'rep'), route)  0.7 us
  transfers between devices with their start and end apart: 10, of which 3 were waited for; matrix products, arithmetic and copies ran while one was open for 0% of the time, Pallas kernels for 6%

profile of v1, /device:TPU:1, one launch (start us, length us, event | category | flops | bytes accessed | tf_op | source)
XLA Modules:
  0.0 33.1 jit_solution(4761870713550087582)
XLA Ops:
  0.6 1.1 %pack.1 = (f32[6,64,128]{2,1,0:T(8,128)S(1)}, f32[2,2,4,8,128]{4,3,2,1,0:T(8,128)S(1)}, f32[2,2,4,8,128]{4,3,2,1,0:T(8,128)S(1)}) custom-call(s32[8,8]{1,0:T(8,128)} %bitcast.11, s32[1,8]{1,0:T(1,128)} %bitcast.12, f32[3,64,128]{2,1,0:T(8,128)} %bitcast.8, f32[3,64,128]{2,1,0:T(8,128)} %bitcast.9, s32[8,8,128]{2,1,0:T(8,128)} %bitcast.10), custom_call_target="tpu_custom_call" | custom-call | tf_op jit(solution)/shard_map/pack/pallas_call | solution.py:171
  1.7 2.1 %collective-permute-start = (f32[6,64,128]{2,1,0:T(8,128)S(1)}, f32[6,64,128]{2,1,0:T(8,128)S(1)}, u32[]{:S(2)}, u32[]{:S(2)}) collective-permute-start(f32[6,64,128]{2,1,0:T(8,128)S(1)} %get-tuple-element.21.table_ref), channel_id=1, source_target_pairs={{0,8},{1,9},{2,10},{3,11},{4,12},{5,13},{6,14},{7,15},{8,16},{9,17... | collective-permute-start | bytes 589832 | tf_op jit(solution)/shard_map/ppermute | solution.py:24
  3.8 1.3 %collective-permute-start.1 = (f32[2,2,4,8,128]{4,3,2,1,0:T(8,128)S(1)}, f32[2,2,4,8,128]{4,3,2,1,0:T(8,128)S(1)}, u32[]{:S(2)}, u32[]{:S(2)}) collective-permute-start(f32[2,2,4,8,128]{4,3,2,1,0:T(8,128)S(1)} %get-tuple-element.23), channel_id=1, source_target_pairs={{0,1},{1,0},{2,3},{3,2},{4,5},{5,4},{6,7},{7,6},{8,9},{9,8},{10,11... | collective-permute-start | bytes 196616 | tf_op jit(solution)/shard_map/ppermute | solution.py:28
  5.1 0.9 %collective-permute-done.1.other_ref = f32[2,2,4,8,128]{4,3,2,1,0:T(8,128)S(1)} collective-permute-done((f32[2,2,4,8,128]{4,3,2,1,0:T(8,128)S(1)}, f32[2,2,4,8,128]{4,3,2,1,0:T(8,128)S(1)}, u32[]{:S(2)}, u32[]{:S(2)}) %collective-permute-start.1) | collective-permute-done | bytes 65568 | tf_op jit(solution)/shard_map/ppermute | solution.py:28
  6.0 7.1 %collective-permute-start.2 = (f32[2,4,16,128]{3,2,1,0:T(8,128)S(1)}, f32[2,4,16,128]{3,2,1,0:T(8,128)S(1)}, u32[]{:S(2)}, u32[]{:S(2)}) collective-permute-start(f32[2,4,16,128]{3,2,1,0:T(8,128)S(1)} %get-tuple-element.24), channel_id=1, source_target_pairs={{0,248},{1,251},{2,250},{3,253},{4,252},{5,255},{6,254},{7,1},{8,0... | collective-permute-start | bytes 196616 | tf_op jit(solution)/shard_map/ppermute | solution.py:24
  13.2 4.0 %collective-permute-start.4 = (f32[2,4,16,128]{3,2,1,0:T(8,128)S(1)}, f32[2,4,16,128]{3,2,1,0:T(8,128)S(1)}, u32[]{:S(2)}, u32[]{:S(2)}) collective-permute-start(f32[2,4,16,128]{3,2,1,0:T(8,128)S(1)} %get-tuple-element.28), channel_id=1, source_target_pairs={{0,254},{1,253},{2,0},{3,255},{4,2},{5,1},{6,4},{7,3},{8,6},{9,5},... | collective-permute-start | bytes 196616 | tf_op jit(solution)/shard_map/ppermute | solution.py:24
  17.1 0.0 collective-permute-done.2.message_ref
  17.1 1.0 %pair.4 = (f32[2,128]{1,0:T(2,128)S(1)}, f32[4,128]{1,0:T(4,128)S(1)}) custom-call(f32[6,64,128]{2,1,0:T(8,128)S(1)} %get-tuple-element.21.table_ref, f32[2,4,16,128]{3,2,1,0:T(8,128)S(1)} %collective-permute-done.2.message_ref), custom_call_target="tpu_custom_call" | custom-call | tf_op jit(solution)/shard_map/pair/pallas_call | solution.py:199
  18.2 0.0 collective-permute-done.table_ref
  18.2 1.0 %pair.5 = (f32[4,128]{1,0:T(4,128)S(1)}, f32[4,128]{1,0:T(4,128)S(1)}) custom-call(f32[6,64,128]{2,1,0:T(8,128)S(1)} %collective-permute-done.table_ref, f32[2,4,16,128]{3,2,1,0:T(8,128)S(1)} %collective-permute-done.2.message_ref, f32[4,128]{1,0:T(4,128)S(1)} %get-tuple-element.25.refs_0_, f32[2,128]{1,0:T(2,128)S(1)} %get-tuple-element.26.refs_1_), custom_call_target="tpu_custom_call" | custom-call | tf_op jit(solution)/shard_map/pair/pallas_call | solution.py:199
  19.3 0.0 collective-permute-done.4.message_ref
  19.3 1.0 %pair.6 = (f32[2,128]{1,0:T(2,128)S(1)}, f32[4,128]{1,0:T(4,128)S(1)}) custom-call(f32[6,64,128]{2,1,0:T(8,128)S(1)} %get-tuple-element.21.table_ref, f32[2,4,16,128]{3,2,1,0:T(8,128)S(1)} %collective-permute-done.4.message_ref, f32[4,128]{1,0:T(4,128)S(1)} %get-tuple-element.29.refs_0_), custom_call_target="tpu_custom_call" | custom-call | tf_op jit(solution)/shard_map/pair/pallas_call | solution.py:199
  20.3 1.0 %pair.7 = (f32[4,128]{1,0:T(4,128)S(1)}, f32[4,128]{1,0:T(4,128)S(1)}) custom-call(f32[6,64,128]{2,1,0:T(8,128)S(1)} %collective-permute-done.table_ref, f32[2,4,16,128]{3,2,1,0:T(8,128)S(1)} %collective-permute-done.4.message_ref, f32[4,128]{1,0:T(4,128)S(1)} %get-tuple-element.30.refs_0_, f32[2,128]{1,0:T(2,128)S(1)} %get-tuple-element.31.refs_1_), custom_call_target="tpu_custom_call" | custom-call | tf_op jit(solution)/shard_map/pair/pallas_call | solution.py:199
  21.4 2.6 %collective-permute-start.5 = (f32[4,128]{1,0:T(4,128)S(1)}, f32[4,128]{1,0:T(4,128)S(1)}, u32[]{:S(2)}, u32[]{:S(2)}) collective-permute-start(f32[4,128]{1,0:T(4,128)S(1)} %get-tuple-element.32), channel_id=1, source_target_pairs={{0,2},{1,5},{2,4},{3,7},{4,6},{5,9},{6,8},{7,11},{8,10},{9,13},{10... | collective-permute-start | bytes 6152 | tf_op jit(solution)/shard_map/ppermute | solution.py:24
  24.0 0.0 collective-permute-start.3
  24.0 5.0 %collective-permute-start.8 = (f32[2,128]{1,0:T(2,128)S(1)}, f32[2,128]{1,0:T(2,128)S(1)}, u32[]{:S(2)}, u32[]{:S(2)}) collective-permute-start(f32[2,128]{1,0:T(2,128)S(1)} %get-tuple-element.35), channel_id=1, source_target_pairs={{0,248},{1,249},{2,250},{3,251},{4,252},{5,253},{6,254},{7,255},{8... | collective-permute-start | bytes 3080 | tf_op jit(solution)/shard_map/ppermute | solution.py:24
  29.0 0.7 %collective-permute-done.5.refs_1_ = f32[4,128]{1,0:T(4,128)S(1)} collective-permute-done((f32[4,128]{1,0:T(4,128)S(1)}, f32[4,128]{1,0:T(4,128)S(1)}, u32[]{:S(2)}, u32[]{:S(2)}) %collective-permute-start.5) | collective-permute-done | bytes 2080 | tf_op jit(solution)/shard_map/ppermute | solution.py:24
  29.6 1.5 %collective-permute-start.7 = (f32[4,128]{1,0:T(4,128)S(1)}, f32[4,128]{1,0:T(4,128)S(1)}, u32[]{:S(2)}, u32[]{:S(2)}) collective-permute-start(f32[4,128]{1,0:T(4,128)S(1)} %collective-permute-done.5.refs_1_), channel_id=1, source_target_pairs={{0,1},{1,0},{2,3},{3,2},{4,5},{5,4},{6,7},{7,6},{8,9},{9,8},{10,11... | collective-permute-start | bytes 6152 | tf_op jit(solution)/shard_map/ppermute | solution.py:28
  31.1 0.0 collective-permute-done.3.refs_0_
  31.1 0.0 collective-permute-start.6
  31.1 0.0 collective-permute-done.8.far_ref
  31.1 0.5 %collective-permute-start.9 = (f32[2,128]{1,0:T(2,128)S(1)}, f32[2,128]{1,0:T(2,128)S(1)}, u32[]{:S(2)}, u32[]{:S(2)}) collective-permute-start(f32[2,128]{1,0:T(2,128)S(1)} %join.1.refs_4_), channel_id=1, source_target_pairs={{0,1},{1,0},{2,3},{3,2},{4,5},{5,4},{6,7},{7,6},{8,9},{9,8},{10,11... | collective-permute-start | bytes 3080 | tf_op jit(solution)/shard_map/ppermute | solution.py:28
  31.6 0.8 %collective-permute-done.9.refs_5_ = f32[2,128]{1,0:T(2,128)S(1)} collective-permute-done((f32[2,128]{1,0:T(2,128)S(1)}, f32[2,128]{1,0:T(2,128)S(1)}, u32[]{:S(2)}, u32[]{:S(2)}) %collective-permute-start.9) | collective-permute-done | bytes 1056 | tf_op jit(solution)/shard_map/ppermute | solution.py:28
  32.4 0.0 collective-permute-done.7.refs_3_
  32.4 0.0 collective-permute-done.6.refs_2_
  32.4 0.6 %finish.1 = (f32[1,36]{1,0:T(1,128)}, f32[1,6]{1,0:T(1,128)}, f32[8,36]{1,0:T(8,128)}) custom-call(f32[4,128]{1,0:T(4,128)S(1)} %collective-permute-done.3.refs_0_, f32[4,128]{1,0:T(4,128)S(1)} %collective-permute-done.5.refs_1_, f32[4,128]{1,0:T(4,128)S(1)} %collective-permute-done.6.refs_2_, f32[4,128]{1,0:T(4,128)S(1)} %collective-permute-done.7.refs_3_, ...), custom_call_target="tpu_custom_call" | custom-call | tf_op jit(solution)/shard_map/finish/pallas_call | solution.py:221
  (3 shorter events, 0.0 us)
Async XLA Ops:
  1.7 16.5 %collective-permute-start = (f32[6,64,128]{2,1,0:T(8,128)S(1)}, f32[6,64,128]{2,1,0:T(8,128)S(1)}, u32[]{:S(2)}, u32[]{:S(2)}) collective-permute-start(f32[6,64,128]{2,1,0:T(8,128)S(1)} %get-tuple-element.21.table_ref), channel_id=1, source_target_pairs={{0,8},{1,9},{2,10},{3,11},{4,12},{5,13},{6,14},{7,15},{8,16},{9,17... | collective-permute-start | bytes 589832 | tf_op jit(solution)/shard_map/ppermute | solution.py:24
  3.8 2.2 %collective-permute-start.1 = (f32[2,2,4,8,128]{4,3,2,1,0:T(8,128)S(1)}, f32[2,2,4,8,128]{4,3,2,1,0:T(8,128)S(1)}, u32[]{:S(2)}, u32[]{:S(2)}) collective-permute-start(f32[2,2,4,8,128]{4,3,2,1,0:T(8,128)S(1)} %get-tuple-element.23), channel_id=1, source_target_pairs={{0,1},{1,0},{2,3},{3,2},{4,5},{5,4},{6,7},{7,6},{8,9},{9,8},{10,11... | collective-permute-start | bytes 196616 | tf_op jit(solution)/shard_map/ppermute | solution.py:28
  6.0 11.1 %collective-permute-start.2 = (f32[2,4,16,128]{3,2,1,0:T(8,128)S(1)}, f32[2,4,16,128]{3,2,1,0:T(8,128)S(1)}, u32[]{:S(2)}, u32[]{:S(2)}) collective-permute-start(f32[2,4,16,128]{3,2,1,0:T(8,128)S(1)} %get-tuple-element.24), channel_id=1, source_target_pairs={{0,248},{1,251},{2,250},{3,253},{4,252},{5,255},{6,254},{7,1},{8,0... | collective-permute-start | bytes 196616 | tf_op jit(solution)/shard_map/ppermute | solution.py:24
  13.2 6.1 %collective-permute-start.4 = (f32[2,4,16,128]{3,2,1,0:T(8,128)S(1)}, f32[2,4,16,128]{3,2,1,0:T(8,128)S(1)}, u32[]{:S(2)}, u32[]{:S(2)}) collective-permute-start(f32[2,4,16,128]{3,2,1,0:T(8,128)S(1)} %get-tuple-element.28), channel_id=1, source_target_pairs={{0,254},{1,253},{2,0},{3,255},{4,2},{5,1},{6,4},{7,3},{8,6},{9,5},... | collective-permute-start | bytes 196616 | tf_op jit(solution)/shard_map/ppermute | solution.py:24
  21.4 8.3 %collective-permute-start.5 = (f32[4,128]{1,0:T(4,128)S(1)}, f32[4,128]{1,0:T(4,128)S(1)}, u32[]{:S(2)}, u32[]{:S(2)}) collective-permute-start(f32[4,128]{1,0:T(4,128)S(1)} %get-tuple-element.32), channel_id=1, source_target_pairs={{0,2},{1,5},{2,4},{3,7},{4,6},{5,9},{6,8},{7,11},{8,10},{9,13},{10... | collective-permute-start | bytes 6152 | tf_op jit(solution)/shard_map/ppermute | solution.py:24
  24.0 7.1 %collective-permute-start.3 = (f32[4,128]{1,0:T(4,128)S(1)}, f32[4,128]{1,0:T(4,128)S(1)}, u32[]{:S(2)}, u32[]{:S(2)}) collective-permute-start(f32[4,128]{1,0:T(4,128)S(1)} %get-tuple-element.27), channel_id=1, source_target_pairs={{0,8},{1,7},{2,10},{3,9},{4,12},{5,11},{6,14},{7,13},{8,16},{9,15}... | collective-permute-start | bytes 6152 | tf_op jit(solution)/shard_map/ppermute | solution.py:24
  24.0 7.1 %collective-permute-start.8 = (f32[2,128]{1,0:T(2,128)S(1)}, f32[2,128]{1,0:T(2,128)S(1)}, u32[]{:S(2)}, u32[]{:S(2)}) collective-permute-start(f32[2,128]{1,0:T(2,128)S(1)} %get-tuple-element.35), channel_id=1, source_target_pairs={{0,248},{1,249},{2,250},{3,251},{4,252},{5,253},{6,254},{7,255},{8... | collective-permute-start | bytes 3080 | tf_op jit(solution)/shard_map/ppermute | solution.py:24
  29.6 2.8 %collective-permute-start.7 = (f32[4,128]{1,0:T(4,128)S(1)}, f32[4,128]{1,0:T(4,128)S(1)}, u32[]{:S(2)}, u32[]{:S(2)}) collective-permute-start(f32[4,128]{1,0:T(4,128)S(1)} %collective-permute-done.5.refs_1_), channel_id=1, source_target_pairs={{0,1},{1,0},{2,3},{3,2},{4,5},{5,4},{6,7},{7,6},{8,9},{9,8},{10,11... | collective-permute-start | bytes 6152 | tf_op jit(solution)/shard_map/ppermute | solution.py:28
  31.1 1.3 %collective-permute-start.6 = (f32[4,128]{1,0:T(4,128)S(1)}, f32[4,128]{1,0:T(4,128)S(1)}, u32[]{:S(2)}, u32[]{:S(2)}) collective-permute-start(f32[4,128]{1,0:T(4,128)S(1)} %collective-permute-done.3.refs_0_), channel_id=1, source_target_pairs={{0,1},{1,0},{2,3},{3,2},{4,5},{5,4},{6,7},{7,6},{8,9},{9,8},{10,11... | collective-permute-start | bytes 6152 | tf_op jit(solution)/shard_map/ppermute | solution.py:28
  31.1 1.3 %collective-permute-start.9 = (f32[2,128]{1,0:T(2,128)S(1)}, f32[2,128]{1,0:T(2,128)S(1)}, u32[]{:S(2)}, u32[]{:S(2)}) collective-permute-start(f32[2,128]{1,0:T(2,128)S(1)} %join.1.refs_4_), channel_id=1, source_target_pairs={{0,1},{1,0},{2,3},{3,2},{4,5},{5,4},{6,7},{7,6},{8,9},{9,8},{10,11... | collective-permute-start | bytes 3080 | tf_op jit(solution)/shard_map/ppermute | solution.py:28

commit v2 on v0

--- a/solution.py
+++ b/solution.py
@@ -19,8 +19,8 @@
 SMEM = pl.BlockSpec(memory_space=pltpu.SMEM)
 
 
-def routed(block, blk, shifts):
-    route = [(i * 2 + r, (i + shifts[r]) % blk * 2 + r) for i in range(blk) for r in range(2)]
+def routed(block, blk, shifts, cross=False):
+    route = [(i * 2 + r, (i + shifts[r]) % blk * 2 + (1 - r if cross else r)) for i in range(blk) for r in range(2)]
     return lax.ppermute(block, ("blk", "rep"), route)
 
 
@@ -49,7 +49,7 @@
 
 
 def step_of(m, rep):
-    return rep if m else 3 - rep
+    return 2 * m + rep
 
 
 def pack_kernel(src_ref, active_ref, points_ref, normals_ref, index_ref, table_ref, *outs):
@@ -186,8 +186,10 @@
         out_shape=[pltpu.VMEM((2, 4, NB, LANES), f32)] * 2,
         name="merge",
     )(near(own), near(other))
-    there = [routed(x, blk, tuple(-s for s in step)) for x, step in zip(messages, steps)]
-    back, totals = [], []
+    there = []
+    for x, step in zip(messages, steps):
+        there.append(routed(x, blk, tuple(-s for s in step)))
+    back, others, totals = [], [], []
     for message, step in zip(there, steps):
         rows = []
         for far in range(2):
@@ -202,6 +204,7 @@
             )(*map(near, args))
             totals = [last]
         back.append(routed(rows[0], blk, step))
+        others.append(routed(rows[0], blk, step, cross=True))
     other_total = swapped(totals[0])
     here_total, far_total = pl.pallas_call(
         join_kernel,
@@ -211,9 +214,6 @@
         name="join",
     )(near(totals[0]), near(other_total))
     far_total = routed(far_total, blk, (-FAR, -FAR))
-    others = []
-    for x in back:
-        others.append(swapped(x))
     diag, grad, pairs = pl.pallas_call(
         functools.partial(finish_kernel, scale=1.0 / (2.0 * rounds)),
         in_specs=[VMEM] * 6,

time: 34.4 us -> 33 us (0.959)
  the two profiles are of different devices: /device:TPU:1 before, /device:TPU:111 now
where the time goes in v2:
time: 33 us; the launch traced here: 32.9 us
  starting transfers between devices  13.2 us (40%)
  waiting for transfers between devices  13.1 us (40%)
  Pallas kernels  5.87 us (18%)
  between operations  0.71 us (2%)
    ppermute x8, waiting for transfers between devices, routed(): return lax.ppermute(block, ('blk', 'rep'), route)  12.2 us
    ppermute x8, starting transfers between devices, routed(): return lax.ppermute(block, ('blk', 'rep'), route)  9.99 us
    pallas_call x4, Pallas kernels, body(): pl.pallas_call(functools.partial(pair_kernel, far=far), in_specs=[VMEM] *...  4.16 us
    ppermute x2, starting transfers between devices, swapped(): return lax.ppermute(block, 'rep', [(0, 1), (1, 0)])  3.22 us
    pallas_call x1, Pallas kernels, body(): pl.pallas_call(pack_kernel, in_specs=[SMEM, SMEM, VMEM, VMEM, VMEM], out_...  1.08 us
    ppermute x2, waiting for transfers between devices, swapped(): return lax.ppermute(block, 'rep', [(0, 1), (1, 0)])  0.9 us
  transfers between devices with their start and end apart: 10, of which 5 were waited for; matrix products, arithmetic and copies ran while one was open for 0% of the time, Pallas kernels for 6%

profile of v2, /device:TPU:111, one launch (start us, length us, event | category | flops | bytes accessed | tf_op | source)
XLA Modules:
  0.0 32.9 jit_solution(11692978456258208535)
XLA Ops:
  0.6 1.1 %pack.1 = (f32[6,64,128]{2,1,0:T(8,128)S(1)}, f32[2,2,4,8,128]{4,3,2,1,0:T(8,128)S(1)}, f32[2,2,4,8,128]{4,3,2,1,0:T(8,128)S(1)}) custom-call(s32[8,8]{1,0:T(8,128)} %bitcast.11, s32[1,8]{1,0:T(1,128)} %bitcast.12, f32[3,64,128]{2,1,0:T(8,128)} %bitcast.8, f32[3,64,128]{2,1,0:T(8,128)} %bitcast.9, s32[8,8,128]{2,1,0:T(8,128)} %bitcast.10), custom_call_target="tpu_custom_call" | custom-call | tf_op jit(solution)/shard_map/pack/pallas_call | solution.py:167
  1.7 2.8 %collective-permute-start = (f32[6,64,128]{2,1,0:T(8,128)S(1)}, f32[6,64,128]{2,1,0:T(8,128)S(1)}, u32[]{:S(2)}, u32[]{:S(2)}) collective-permute-start(f32[6,64,128]{2,1,0:T(8,128)S(1)} %get-tuple-element.21.table_ref), channel_id=1, source_target_pairs={{0,8},{1,9},{2,10},{3,11},{4,12},{5,13},{6,14},{7,15},{8,16},{9,17... | collective-permute-start | bytes 589832 | tf_op jit(solution)/shard_map/ppermute | solution.py:24
  4.6 1.0 %collective-permute-start.1 = (f32[2,2,4,8,128]{4,3,2,1,0:T(8,128)S(1)}, f32[2,2,4,8,128]{4,3,2,1,0:T(8,128)S(1)}, u32[]{:S(2)}, u32[]{:S(2)}) collective-permute-start(f32[2,2,4,8,128]{4,3,2,1,0:T(8,128)S(1)} %get-tuple-element.23), channel_id=1, source_target_pairs={{0,1},{1,0},{2,3},{3,2},{4,5},{5,4},{6,7},{7,6},{8,9},{9,8},{10,11... | collective-permute-start | bytes 196616 | tf_op jit(solution)/shard_map/ppermute | solution.py:28
  5.5 0.9 %collective-permute-done.1.other_ref = f32[2,2,4,8,128]{4,3,2,1,0:T(8,128)S(1)} collective-permute-done((f32[2,2,4,8,128]{4,3,2,1,0:T(8,128)S(1)}, f32[2,2,4,8,128]{4,3,2,1,0:T(8,128)S(1)}, u32[]{:S(2)}, u32[]{:S(2)}) %collective-permute-start.1) | collective-permute-done | bytes 65568 | tf_op jit(solution)/shard_map/ppermute | solution.py:28
  6.4 0.5 %collective-permute-start.2 = (f32[2,4,16,128]{3,2,1,0:T(8,128)S(1)}, f32[2,4,16,128]{3,2,1,0:T(8,128)S(1)}, u32[]{:S(2)}, u32[]{:S(2)}) collective-permute-start(f32[2,4,16,128]{3,2,1,0:T(8,128)S(1)} %get-tuple-element.24), channel_id=1, source_target_pairs={{0,254},{1,253},{2,0},{3,255},{4,2},{5,1},{6,4},{7,3},{8,6},{9,5},... | collective-permute-start | bytes 196616 | tf_op jit(solution)/shard_map/ppermute | solution.py:24
  6.9 0.5 %collective-permute-start.4 = (f32[2,4,16,128]{3,2,1,0:T(8,128)S(1)}, f32[2,4,16,128]{3,2,1,0:T(8,128)S(1)}, u32[]{:S(2)}, u32[]{:S(2)}) collective-permute-start(f32[2,4,16,128]{3,2,1,0:T(8,128)S(1)} %get-tuple-element.28), channel_id=1, source_target_pairs={{0,250},{1,249},{2,252},{3,251},{4,254},{5,253},{6,0},{7,255},{8,2... | collective-permute-start | bytes 196616 | tf_op jit(solution)/shard_map/ppermute | solution.py:24
  7.5 4.0 %collective-permute-done.2.message_ref = f32[2,4,16,128]{3,2,1,0:T(8,128)S(1)} collective-permute-done((f32[2,4,16,128]{3,2,1,0:T(8,128)S(1)}, f32[2,4,16,128]{3,2,1,0:T(8,128)S(1)}, u32[]{:S(2)}, u32[]{:S(2)}) %collective-permute-start.2) | collective-permute-done | bytes 65568 | tf_op jit(solution)/shard_map/ppermute | solution.py:24
  11.5 1.0 %pair.4 = (f32[2,128]{1,0:T(2,128)S(1)}, f32[4,128]{1,0:T(4,128)S(1)}) custom-call(f32[6,64,128]{2,1,0:T(8,128)S(1)} %get-tuple-element.21.table_ref, f32[2,4,16,128]{3,2,1,0:T(8,128)S(1)} %collective-permute-done.2.message_ref), custom_call_target="tpu_custom_call" | custom-call | tf_op jit(solution)/shard_map/pair/pallas_call | solution.py:197
  12.5 0.0 collective-permute-done.table_ref
  12.6 1.0 %pair.5 = (f32[4,128]{1,0:T(4,128)S(1)}, f32[4,128]{1,0:T(4,128)S(1)}) custom-call(f32[6,64,128]{2,1,0:T(8,128)S(1)} %collective-permute-done.table_ref, f32[2,4,16,128]{3,2,1,0:T(8,128)S(1)} %collective-permute-done.2.message_ref, f32[4,128]{1,0:T(4,128)S(1)} %get-tuple-element.25.refs_0_, f32[2,128]{1,0:T(2,128)S(1)} %get-tuple-element.26.refs_1_), custom_call_target="tpu_custom_call" | custom-call | tf_op jit(solution)/shard_map/pair/pallas_call | solution.py:197
  13.6 2.5 %collective-permute-done.4.message_ref = f32[2,4,16,128]{3,2,1,0:T(8,128)S(1)} collective-permute-done((f32[2,4,16,128]{3,2,1,0:T(8,128)S(1)}, f32[2,4,16,128]{3,2,1,0:T(8,128)S(1)}, u32[]{:S(2)}, u32[]{:S(2)}) %collective-permute-start.4) | collective-permute-done | bytes 65568 | tf_op jit(solution)/shard_map/ppermute | solution.py:24
  16.1 1.0 %pair.6 = (f32[2,128]{1,0:T(2,128)S(1)}, f32[4,128]{1,0:T(4,128)S(1)}) custom-call(f32[6,64,128]{2,1,0:T(8,128)S(1)} %get-tuple-element.21.table_ref, f32[2,4,16,128]{3,2,1,0:T(8,128)S(1)} %collective-permute-done.4.message_ref, f32[4,128]{1,0:T(4,128)S(1)} %get-tuple-element.29.refs_0_), custom_call_target="tpu_custom_call" | custom-call | tf_op jit(solution)/shard_map/pair/pallas_call | solution.py:197
  17.1 1.0 %pair.7 = (f32[4,128]{1,0:T(4,128)S(1)}, f32[4,128]{1,0:T(4,128)S(1)}) custom-call(f32[6,64,128]{2,1,0:T(8,128)S(1)} %collective-permute-done.table_ref, f32[2,4,16,128]{3,2,1,0:T(8,128)S(1)} %collective-permute-done.4.message_ref, f32[4,128]{1,0:T(4,128)S(1)} %get-tuple-element.30.refs_0_, f32[2,128]{1,0:T(2,128)S(1)} %get-tuple-element.31.refs_1_), custom_call_target="tpu_custom_call" | custom-call | tf_op jit(solution)/shard_map/pair/pallas_call | solution.py:197
  18.2 2.3 %collective-permute-start.8 = (f32[4,128]{1,0:T(4,128)S(1)}, f32[4,128]{1,0:T(4,128)S(1)}, u32[]{:S(2)}, u32[]{:S(2)}) collective-permute-start(f32[4,128]{1,0:T(4,128)S(1)} %get-tuple-element.33.own_ref), channel_id=1, source_target_pairs={{0,1},{1,0},{2,3},{3,2},{4,5},{5,4},{6,7},{7,6},{8,9},{9,8},{10,11... | collective-permute-start | bytes 6152 | tf_op jit(solution)/shard_map/ppermute | solution.py:28
  20.4 0.0 collective-permute-start.7
  20.4 0.0 collective-permute-start.5
  20.4 3.3 %collective-permute-start.6 = (f32[4,128]{1,0:T(4,128)S(1)}, f32[4,128]{1,0:T(4,128)S(1)}, u32[]{:S(2)}, u32[]{:S(2)}) collective-permute-start(f32[4,128]{1,0:T(4,128)S(1)} %get-tuple-element.27), channel_id=1, source_target_pairs={{0,3},{1,4},{2,5},{3,6},{4,7},{5,8},{6,9},{7,10},{8,11},{9,12},{10... | collective-permute-start | bytes 6152 | tf_op jit(solution)/shard_map/ppermute | solution.py:24
  23.7 2.8 %collective-permute-start.3 = (f32[4,128]{1,0:T(4,128)S(1)}, f32[4,128]{1,0:T(4,128)S(1)}, u32[]{:S(2)}, u32[]{:S(2)}) collective-permute-start(f32[4,128]{1,0:T(4,128)S(1)} %get-tuple-element.27), channel_id=1, source_target_pairs={{0,2},{1,5},{2,4},{3,7},{4,6},{5,9},{6,8},{7,11},{8,10},{9,13},{10... | collective-permute-start | bytes 6152 | tf_op jit(solution)/shard_map/ppermute | solution.py:24
  26.5 0.0 collective-permute-done.8.other_ref
  26.5 0.0 collective-permute-start.9
  26.5 0.0 collective-permute-done.7.refs_3_
  26.6 0.0 collective-permute-done.5.refs_1_
  26.6 0.0 collective-permute-done.6.refs_2_
  26.6 2.0 %collective-permute-done.3.refs_0_ = f32[4,128]{1,0:T(4,128)S(1)} collective-permute-done((f32[4,128]{1,0:T(4,128)S(1)}, f32[4,128]{1,0:T(4,128)S(1)}, u32[]{:S(2)}, u32[]{:S(2)}) %collective-permute-start.3) | collective-permute-done | bytes 2080 | tf_op jit(solution)/shard_map/ppermute | solution.py:24
  28.6 3.7 %collective-permute-done.9.refs_5_ = f32[2,128]{1,0:T(2,128)S(1)} collective-permute-done((f32[2,128]{1,0:T(2,128)S(1)}, f32[2,128]{1,0:T(2,128)S(1)}, u32[]{:S(2)}, u32[]{:S(2)}) %collective-permute-start.9) | collective-permute-done | bytes 1056 | tf_op jit(solution)/shard_map/ppermute | solution.py:24
  32.3 0.6 %finish.1 = (f32[1,36]{1,0:T(1,128)}, f32[1,6]{1,0:T(1,128)}, f32[8,36]{1,0:T(8,128)}) custom-call(f32[4,128]{1,0:T(4,128)S(1)} %collective-permute-done.3.refs_0_, f32[4,128]{1,0:T(4,128)S(1)} %collective-permute-done.5.refs_1_, f32[4,128]{1,0:T(4,128)S(1)} %collective-permute-done.6.refs_2_, f32[4,128]{1,0:T(4,128)S(1)} %collective-permute-done.7.refs_3_, ...), custom_call_target="tpu_custom_call" | custom-call | tf_op jit(solution)/shard_map/finish/pallas_call | solution.py:217
  (2 shorter events, 0.0 us)
Async XLA Ops:
  1.7 10.8 %collective-permute-start = (f32[6,64,128]{2,1,0:T(8,128)S(1)}, f32[6,64,128]{2,1,0:T(8,128)S(1)}, u32[]{:S(2)}, u32[]{:S(2)}) collective-permute-start(f32[6,64,128]{2,1,0:T(8,128)S(1)} %get-tuple-element.21.table_ref), channel_id=1, source_target_pairs={{0,8},{1,9},{2,10},{3,11},{4,12},{5,13},{6,14},{7,15},{8,16},{9,17... | collective-permute-start | bytes 589832 | tf_op jit(solution)/shard_map/ppermute | solution.py:24
  4.6 1.9 %collective-permute-start.1 = (f32[2,2,4,8,128]{4,3,2,1,0:T(8,128)S(1)}, f32[2,2,4,8,128]{4,3,2,1,0:T(8,128)S(1)}, u32[]{:S(2)}, u32[]{:S(2)}) collective-permute-start(f32[2,2,4,8,128]{4,3,2,1,0:T(8,128)S(1)} %get-tuple-element.23), channel_id=1, source_target_pairs={{0,1},{1,0},{2,3},{3,2},{4,5},{5,4},{6,7},{7,6},{8,9},{9,8},{10,11... | collective-permute-start | bytes 196616 | tf_op jit(solution)/shard_map/ppermute | solution.py:28
  6.4 5.1 %collective-permute-start.2 = (f32[2,4,16,128]{3,2,1,0:T(8,128)S(1)}, f32[2,4,16,128]{3,2,1,0:T(8,128)S(1)}, u32[]{:S(2)}, u32[]{:S(2)}) collective-permute-start(f32[2,4,16,128]{3,2,1,0:T(8,128)S(1)} %get-tuple-element.24), channel_id=1, source_target_pairs={{0,254},{1,253},{2,0},{3,255},{4,2},{5,1},{6,4},{7,3},{8,6},{9,5},... | collective-permute-start | bytes 196616 | tf_op jit(solution)/shard_map/ppermute | solution.py:24
  6.9 9.1 %collective-permute-start.4 = (f32[2,4,16,128]{3,2,1,0:T(8,128)S(1)}, f32[2,4,16,128]{3,2,1,0:T(8,128)S(1)}, u32[]{:S(2)}, u32[]{:S(2)}) collective-permute-start(f32[2,4,16,128]{3,2,1,0:T(8,128)S(1)} %get-tuple-element.28), channel_id=1, source_target_pairs={{0,250},{1,249},{2,252},{3,251},{4,254},{5,253},{6,0},{7,255},{8,2... | collective-permute-start | bytes 196616 | tf_op jit(solution)/shard_map/ppermute | solution.py:24
  18.2 8.4 %collective-permute-start.8 = (f32[4,128]{1,0:T(4,128)S(1)}, f32[4,128]{1,0:T(4,128)S(1)}, u32[]{:S(2)}, u32[]{:S(2)}) collective-permute-start(f32[4,128]{1,0:T(4,128)S(1)} %get-tuple-element.33.own_ref), channel_id=1, source_target_pairs={{0,1},{1,0},{2,3},{3,2},{4,5},{5,4},{6,7},{7,6},{8,9},{9,8},{10,11... | collective-permute-start | bytes 6152 | tf_op jit(solution)/shard_map/ppermute | solution.py:28
  20.4 6.1 %collective-permute-start.7 = (f32[4,128]{1,0:T(4,128)S(1)}, f32[4,128]{1,0:T(4,128)S(1)}, u32[]{:S(2)}, u32[]{:S(2)}) collective-permute-start(f32[4,128]{1,0:T(4,128)S(1)} %get-tuple-element.32), channel_id=1, source_target_pairs={{0,7},{1,8},{2,9},{3,10},{4,11},{5,12},{6,13},{7,14},{8,15},{9,16}... | collective-permute-start | bytes 6152 | tf_op jit(solution)/shard_map/ppermute | solution.py:24
  20.4 6.1 %collective-permute-start.5 = (f32[4,128]{1,0:T(4,128)S(1)}, f32[4,128]{1,0:T(4,128)S(1)}, u32[]{:S(2)}, u32[]{:S(2)}) collective-permute-start(f32[4,128]{1,0:T(4,128)S(1)} %get-tuple-element.32), channel_id=1, source_target_pairs={{0,6},{1,9},{2,8},{3,11},{4,10},{5,13},{6,12},{7,15},{8,14},{9,17}... | collective-permute-start | bytes 6152 | tf_op jit(solution)/shard_map/ppermute | solution.py:24
  20.4 6.1 %collective-permute-start.6 = (f32[4,128]{1,0:T(4,128)S(1)}, f32[4,128]{1,0:T(4,128)S(1)}, u32[]{:S(2)}, u32[]{:S(2)}) collective-permute-start(f32[4,128]{1,0:T(4,128)S(1)} %get-tuple-element.27), channel_id=1, source_target_pairs={{0,3},{1,4},{2,5},{3,6},{4,7},{5,8},{6,9},{7,10},{8,11},{9,12},{10... | collective-permute-start | bytes 6152 | tf_op jit(solution)/shard_map/ppermute | solution.py:24
  23.7 4.8 %collective-permute-start.3 = (f32[4,128]{1,0:T(4,128)S(1)}, f32[4,128]{1,0:T(4,128)S(1)}, u32[]{:S(2)}, u32[]{:S(2)}) collective-permute-start(f32[4,128]{1,0:T(4,128)S(1)} %get-tuple-element.27), channel_id=1, source_target_pairs={{0,2},{1,5},{2,4},{3,7},{4,6},{5,9},{6,8},{7,11},{8,10},{9,13},{10... | collective-permute-start | bytes 6152 | tf_op jit(solution)/shard_map/ppermute | solution.py:24
  26.5 5.7 %collective-permute-start.9 = (f32[2,128]{1,0:T(2,128)S(1)}, f32[2,128]{1,0:T(2,128)S(1)}, u32[]{:S(2)}, u32[]{:S(2)}) collective-permute-start(f32[2,128]{1,0:T(2,128)S(1)} %get-tuple-element.35), channel_id=1, source_target_pairs={{0,248},{1,249},{2,250},{3,251},{4,252},{5,253},{6,254},{7,255},{8... | collective-permute-start | bytes 3080 | tf_op jit(solution)/shard_map/ppermute | solution.py:24

commit v3 on v1

--- a/solution.py
+++ b/solution.py
@@ -49,7 +49,7 @@
 
 
 def step_of(m, rep):
-    return rep if m else 3 - rep
+    return 3 - m - 2 * rep
 
 
 def pack_kernel(src_ref, active_ref, points_ref, normals_ref, index_ref, table_ref, *outs):
@@ -77,8 +77,11 @@
                 out[far, c, pl.ds(SUBLANES, SUBLANES), :] = other_ref[m, far, c]
 
 
-def pair_kernel(table_ref, message_ref, *refs, far):
-    rows_ref, totals_ref, sums_s = refs[-3:]
+def near_kernel(table_ref, message_ref, sums_ref):
+    pair_sums(table_ref, message_ref, 0, sums_ref)
+
+
+def pair_sums(table_ref, message_ref, far, sums_ref):
     shape = (SUBLANES, LANES)
     index = [message_ref[far, 3, pl.ds(h * SUBLANES, SUBLANES), :].astype(jnp.int32) for h in range(2)]
     lanes = [i & (LANES - 1) for i in index]
@@ -108,35 +111,44 @@
         terms = [scaled[a] * jacob[b] for a in range(6) for b in range(a, 6)]
         terms += [scaled[a] * resid for a in range(6)]
         parts.append(terms)
+    sums_ref[24:32, :] = jnp.zeros(shape, jnp.float32)
     for t in range(27):
-        sums_s[pl.ds(t, 1), :] = jnp.sum(parts[0][t] + parts[1][t], axis=0, keepdims=True)
-
+        sums_ref[pl.ds(t, 1), :] = jnp.sum(parts[0][t] + parts[1][t], axis=0, keepdims=True)
+
+
+def far_kernel(table_ref, message_ref, near_ref, *refs):
+    (previous_ref,) = refs[:-3] or (None,)
+    rows_ref, totals_ref, sums_s = refs[-3:]
+    pair_sums(table_ref, message_ref, 1, sums_s)
+    shape = (SUBLANES, LANES)
     row = lax.broadcasted_iota(jnp.int32, shape, 0)
     lane = lax.broadcasted_iota(jnp.int32, shape, 1)
     first, second = lane // 6, lane % 6
     low, top = jnp.minimum(first, second), jnp.maximum(first, second)
     gram_term = jnp.where(lane < 36, low * (11 - low) // 2 + top, -1)
     push_term = jnp.where(lane < 6, 21 + lane, -1)
-    gram = jnp.zeros(shape, jnp.float32)
-    push = jnp.zeros(shape, jnp.float32)
-    for g in range(4):
-        column = jnp.sum(sums_s[pl.ds(SUBLANES * g, SUBLANES), :], axis=1, keepdims=True)
-        term = SUBLANES * g + row
-        if g < 3:
-            gram = jnp.where(gram_term == term, column, gram)
-        if g > 1:
-            push = jnp.where(push_term == term, column, push)
     scale = 1.0 / (NB * BLOCK)
-    gram = jnp.sum(gram, axis=0, keepdims=True) * scale
-    push = jnp.sum(push, axis=0, keepdims=True) * scale
-    at = 2 * far
-    if far:
-        rows_ref[0:2, :] = refs[1][...]
-    rows_ref[at : at + 1, :] = gram
-    rows_ref[at + 1 : at + 2, :] = push
-    totals_ref[...] = refs[0][...] if len(refs) > 3 else jnp.zeros((4, LANES), jnp.float32)
-    totals_ref[at : at + 1, :] += gram
-    totals_ref[at + 1 : at + 2, :] -= push
+    for far, sums_ref in enumerate((near_ref, sums_s)):
+        gram = jnp.zeros(shape, jnp.float32)
+        push = jnp.zeros(shape, jnp.float32)
+        for g in range(4):
+            column = jnp.sum(sums_ref[pl.ds(SUBLANES * g, SUBLANES), :], axis=1, keepdims=True)
+            term = SUBLANES * g + row
+            if g < 3:
+                gram = jnp.where(gram_term == term, column, gram)
+            if g > 1:
+                push = jnp.where(push_term == term, column, push)
+        gram = jnp.sum(gram, axis=0, keepdims=True) * scale
+        push = jnp.sum(push, axis=0, keepdims=True) * scale
+        at = 2 * far
+        rows_ref[at : at + 1, :] = gram
+        rows_ref[at + 1 : at + 2, :] = push
+        push = -push
+        if previous_ref is not None:
+            gram = previous_ref[at : at + 1, :] + gram
+            push = previous_ref[at + 1 : at + 2, :] + push
+        totals_ref[at : at + 1, :] = gram
+        totals_ref[at + 1 : at + 2, :] = push
 
 
 def split_kernel(totals_ref, here_ref, far_ref):
@@ -190,22 +202,28 @@
         out_shape=[pltpu.VMEM((2, 4, NB, LANES), f32)] * 2,
         name="merge",
     )(near(own), near(other))
-    there = [routed(x, blk, tuple(-s for s in step)) for x, step in zip(messages, steps)]
+    there = []
+    for x, step in zip(messages, steps):
+        there.append(routed(x, blk, tuple(-s for s in step)))
     back, totals = [], []
     for message, step in zip(there, steps):
-        rows = []
-        for far in range(2):
-            args = [far_table if far else table, message, *totals, *rows]
-            *rows, last = pl.pallas_call(
-                functools.partial(pair_kernel, far=far),
-                in_specs=[VMEM] * len(args),
-                out_specs=[VMEM] * 2,
-                out_shape=[pltpu.VMEM((2 + 2 * far, LANES), f32), pltpu.VMEM((4, LANES), f32)],
-                scratch_shapes=[pltpu.VMEM((32, LANES), f32)],
-                name="pair",
-            )(*map(near, args))
-            totals = [last]
-        back.append(routed(rows[0], blk, step))
+        sums = pl.pallas_call(
+            near_kernel,
+            in_specs=[VMEM] * 2,
+            out_specs=VMEM,
+            out_shape=pltpu.VMEM((32, LANES), f32),
+            name="near",
+        )(near(table), near(message))
+        rows, last = pl.pallas_call(
+            far_kernel,
+            in_specs=[VMEM] * (3 + len(totals)),
+            out_specs=[VMEM] * 2,
+            out_shape=[pltpu.VMEM((4, LANES), f32)] * 2,
+            scratch_shapes=[pltpu.VMEM((32, LANES), f32)],
+            name="far",
+        )(*map(near, (far_table, message, sums, *totals)))
+        totals = [last]
+        back.append(routed(rows, blk, step))
     total = pltpu.VMEM((2, LANES), f32)
     here_total, far_total = pl.pallas_call(
         split_kernel, in_specs=[VMEM], out_specs=[VMEM] * 2, out_shape=[total] * 2, name="split"

time: 33.2 us -> 33 us (level)
  starting transfers between devices: 24.1 us -> 22.6 us
  waiting for transfers between devices: 2.43 us -> 3.78 us
    ppermute x6, waiting for transfers between devices: 0.7 us -> 1.8 us  [routed(): return lax.ppermute(block, ('blk', 'rep'), route)]
    ppermute x6, starting transfers between devices: 20.8 us -> 19.8 us  [routed(): return lax.ppermute(block, ('blk', 'rep'), route)]
    ppermute x4, starting transfers between devices: 3.24 us -> 2.85 us  [swapped(): return lax.ppermute(block, 'rep', [(0, 1), (1, 0)])]
  transfers between devices with their start and end apart: 10 -> 10, of which waited for: 3 -> 5; matrix products, arithmetic and copies ran while one was open for 0% -> 0% of each run, Pallas kernels for 6% -> 6%
where the time goes in v3:
time: 33 us; the launch traced here: 32.9 us
  starting transfers between devices  22.6 us (68%)
  Pallas kernels  5.78 us (18%)
  waiting for transfers between devices  3.78 us (11%)
  between operations  0.69 us (2%)
    ppermute x6, starting transfers between devices, routed(): return lax.ppermute(block, ('blk', 'rep'), route)  19.8 us
    ppermute x4, starting transfers between devices, swapped(): return lax.ppermute(block, 'rep', [(0, 1), (1, 0)])  2.85 us
    pallas_call x2, Pallas kernels, body(): pl.pallas_call(far_kernel, in_specs=[VMEM] * (3 + len(totals)), out_specs...  2.12 us
    ppermute x4, waiting for transfers between devices, swapped(): return lax.ppermute(block, 'rep', [(0, 1), (1, 0)])  1.98 us
    pallas_call x2, Pallas kernels, body(): pl.pallas_call(near_kernel, in_specs=[VMEM] * 2, out_specs=VMEM, out_shap...  1.95 us
    ppermute x6, waiting for transfers between devices, routed(): return lax.ppermute(block, ('blk', 'rep'), route)  1.8 us
    pallas_call x1, Pallas kernels, body(): pl.pallas_call(pack_kernel, in_specs=[SMEM, SMEM, VMEM, VMEM, VMEM], out_...  1.08 us
  transfers between devices with their start and end apart: 10, of which 5 were waited for; matrix products, arithmetic and copies ran while one was open for 0% of the time, Pallas kernels for 6%

profile of v3, /device:TPU:1, one launch (start us, length us, event | category | flops | bytes accessed | tf_op | source)
XLA Modules:
  0.0 32.9 jit_solution(1877939645460402724)
XLA Ops:
  0.6 1.1 %pack.1 = (f32[6,64,128]{2,1,0:T(8,128)S(1)}, f32[2,2,4,8,128]{4,3,2,1,0:T(8,128)S(1)}, f32[2,2,4,8,128]{4,3,2,1,0:T(8,128)S(1)}) custom-call(s32[8,8]{1,0:T(8,128)} %bitcast.11, s32[1,8]{1,0:T(1,128)} %bitcast.12, f32[3,64,128]{2,1,0:T(8,128)} %bitcast.8, f32[3,64,128]{2,1,0:T(8,128)} %bitcast.9, s32[8,8,128]{2,1,0:T(8,128)} %bitcast.10), custom_call_target="tpu_custom_call" | custom-call | tf_op jit(solution)/shard_map/pack/pallas_call | solution.py:183
  1.7 2.1 %collective-permute-start = (f32[6,64,128]{2,1,0:T(8,128)S(1)}, f32[6,64,128]{2,1,0:T(8,128)S(1)}, u32[]{:S(2)}, u32[]{:S(2)}) collective-permute-start(f32[6,64,128]{2,1,0:T(8,128)S(1)} %get-tuple-element.17.table_ref), channel_id=1, source_target_pairs={{0,8},{1,9},{2,10},{3,11},{4,12},{5,13},{6,14},{7,15},{8,16},{9,17... | collective-permute-start | bytes 589832 | tf_op jit(solution)/shard_map/ppermute | solution.py:24
  3.8 1.3 %collective-permute-start.1 = (f32[2,2,4,8,128]{4,3,2,1,0:T(8,128)S(1)}, f32[2,2,4,8,128]{4,3,2,1,0:T(8,128)S(1)}, u32[]{:S(2)}, u32[]{:S(2)}) collective-permute-start(f32[2,2,4,8,128]{4,3,2,1,0:T(8,128)S(1)} %get-tuple-element.19), channel_id=1, source_target_pairs={{0,1},{1,0},{2,3},{3,2},{4,5},{5,4},{6,7},{7,6},{8,9},{9,8},{10,11... | collective-permute-start | bytes 196616 | tf_op jit(solution)/shard_map/ppermute | solution.py:28
  5.1 0.9 %collective-permute-done.1.other_ref = f32[2,2,4,8,128]{4,3,2,1,0:T(8,128)S(1)} collective-permute-done((f32[2,2,4,8,128]{4,3,2,1,0:T(8,128)S(1)}, f32[2,2,4,8,128]{4,3,2,1,0:T(8,128)S(1)}, u32[]{:S(2)}, u32[]{:S(2)}) %collective-permute-start.1) | collective-permute-done | bytes 65568 | tf_op jit(solution)/shard_map/ppermute | solution.py:28
  6.0 8.8 %collective-permute-start.2 = (f32[2,4,16,128]{3,2,1,0:T(8,128)S(1)}, f32[2,4,16,128]{3,2,1,0:T(8,128)S(1)}, u32[]{:S(2)}, u32[]{:S(2)}) collective-permute-start(f32[2,4,16,128]{3,2,1,0:T(8,128)S(1)} %get-tuple-element.20), channel_id=1, source_target_pairs={{0,248},{1,253},{2,250},{3,255},{4,252},{5,1},{6,254},{7,3},{8,0},... | collective-permute-start | bytes 196616 | tf_op jit(solution)/shard_map/ppermute | solution.py:24
  14.8 0.8 %collective-permute-start.4 = (f32[2,4,16,128]{3,2,1,0:T(8,128)S(1)}, f32[2,4,16,128]{3,2,1,0:T(8,128)S(1)}, u32[]{:S(2)}, u32[]{:S(2)}) collective-permute-start(f32[2,4,16,128]{3,2,1,0:T(8,128)S(1)} %get-tuple-element.22), channel_id=1, source_target_pairs={{0,250},{1,255},{2,252},{3,1},{4,254},{5,3},{6,0},{7,5},{8,2},{9,7... | collective-permute-start | bytes 196616 | tf_op jit(solution)/shard_map/ppermute | solution.py:24
  15.6 0.6 %collective-permute-done.2.message_ref = f32[2,4,16,128]{3,2,1,0:T(8,128)S(1)} collective-permute-done((f32[2,4,16,128]{3,2,1,0:T(8,128)S(1)}, f32[2,4,16,128]{3,2,1,0:T(8,128)S(1)}, u32[]{:S(2)}, u32[]{:S(2)}) %collective-permute-start.2) | collective-permute-done | bytes 65568 | tf_op jit(solution)/shard_map/ppermute | solution.py:24
  16.1 1.0 %near.2.near_ref = f32[32,128]{1,0:T(8,128)S(1)} custom-call(f32[6,64,128]{2,1,0:T(8,128)S(1)} %get-tuple-element.17.table_ref, f32[2,4,16,128]{3,2,1,0:T(8,128)S(1)} %collective-permute-done.2.message_ref), custom_call_target="tpu_custom_call" | custom-call | tf_op jit(solution)/shard_map/near/pallas_call | solution.py:210
  17.1 0.8 %collective-permute-done.4.message_ref = f32[2,4,16,128]{3,2,1,0:T(8,128)S(1)} collective-permute-done((f32[2,4,16,128]{3,2,1,0:T(8,128)S(1)}, f32[2,4,16,128]{3,2,1,0:T(8,128)S(1)}, u32[]{:S(2)}, u32[]{:S(2)}) %collective-permute-start.4) | collective-permute-done | bytes 65568 | tf_op jit(solution)/shard_map/ppermute | solution.py:24
  17.9 1.0 %near.3.near_ref = f32[32,128]{1,0:T(8,128)S(1)} custom-call(f32[6,64,128]{2,1,0:T(8,128)S(1)} %get-tuple-element.17.table_ref, f32[2,4,16,128]{3,2,1,0:T(8,128)S(1)} %collective-permute-done.4.message_ref), custom_call_target="tpu_custom_call" | custom-call | tf_op jit(solution)/shard_map/near/pallas_call | solution.py:210
  18.9 0.0 collective-permute-done.table_ref
  18.9 1.1 %far.2 = (f32[4,128]{1,0:T(4,128)S(1)}, f32[4,128]{1,0:T(4,128)S(1)}) custom-call(f32[6,64,128]{2,1,0:T(8,128)S(1)} %collective-permute-done.table_ref, f32[2,4,16,128]{3,2,1,0:T(8,128)S(1)} %collective-permute-done.2.message_ref, f32[32,128]{1,0:T(8,128)S(1)} %near.2.near_ref), custom_call_target="tpu_custom_call" | custom-call | tf_op jit(solution)/shard_map/far/pallas_call | solution.py:217
  20.0 1.1 %far.3 = (f32[4,128]{1,0:T(4,128)S(1)}, f32[4,128]{1,0:T(4,128)S(1)}) custom-call(f32[6,64,128]{2,1,0:T(8,128)S(1)} %collective-permute-done.table_ref, f32[2,4,16,128]{3,2,1,0:T(8,128)S(1)} %collective-permute-done.4.message_ref, f32[32,128]{1,0:T(8,128)S(1)} %near.3.near_ref, f32[4,128]{1,0:T(4,128)S(1)} %get-tuple-element.23.refs_0_), custom_call_target="tpu_custom_call" | custom-call | tf_op jit(solution)/shard_map/far/pallas_call | solution.py:217
  21.0 0.8 %collective-permute-start.5 = (f32[4,128]{1,0:T(4,128)S(1)}, f32[4,128]{1,0:T(4,128)S(1)}, u32[]{:S(2)}, u32[]{:S(2)}) collective-permute-start(f32[4,128]{1,0:T(4,128)S(1)} %get-tuple-element.24), channel_id=1, source_target_pairs={{0,6},{1,3},{2,8},{3,5},{4,10},{5,7},{6,12},{7,9},{8,14},{9,11},{1... | collective-permute-start | bytes 6152 | tf_op jit(solution)/shard_map/ppermute | solution.py:24
  21.8 0.0 collective-permute-start.3
  21.8 7.3 %collective-permute-start.8 = (f32[2,128]{1,0:T(2,128)S(1)}, f32[2,128]{1,0:T(2,128)S(1)}, u32[]{:S(2)}, u32[]{:S(2)}) collective-permute-start(f32[2,128]{1,0:T(2,128)S(1)} %get-tuple-element.27), channel_id=1, source_target_pairs={{0,248},{1,249},{2,250},{3,251},{4,252},{5,253},{6,254},{7,255},{8... | collective-permute-start | bytes 3080 | tf_op jit(solution)/shard_map/ppermute | solution.py:24
  29.1 0.0 collective-permute-done.5.refs_1_
  29.2 0.4 %collective-permute-start.7 = (f32[4,128]{1,0:T(4,128)S(1)}, f32[4,128]{1,0:T(4,128)S(1)}, u32[]{:S(2)}, u32[]{:S(2)}) collective-permute-start(f32[4,128]{1,0:T(4,128)S(1)} %collective-permute-done.5.refs_1_), channel_id=1, source_target_pairs={{0,1},{1,0},{2,3},{3,2},{4,5},{5,4},{6,7},{7,6},{8,9},{9,8},{10,11... | collective-permute-start | bytes 6152 | tf_op jit(solution)/shard_map/ppermute | solution.py:28
  29.5 0.4 %collective-permute-done.3.refs_0_ = f32[4,128]{1,0:T(4,128)S(1)} collective-permute-done((f32[4,128]{1,0:T(4,128)S(1)}, f32[4,128]{1,0:T(4,128)S(1)}, u32[]{:S(2)}, u32[]{:S(2)}) %collective-permute-start.3) | collective-permute-done | bytes 2080 | tf_op jit(solution)/shard_map/ppermute | solution.py:24
  30.0 1.1 %collective-permute-start.6 = (f32[4,128]{1,0:T(4,128)S(1)}, f32[4,128]{1,0:T(4,128)S(1)}, u32[]{:S(2)}, u32[]{:S(2)}) collective-permute-start(f32[4,128]{1,0:T(4,128)S(1)} %collective-permute-done.3.refs_0_), channel_id=1, source_target_pairs={{0,1},{1,0},{2,3},{3,2},{4,5},{5,4},{6,7},{7,6},{8,9},{9,8},{10,11... | collective-permute-start | bytes 6152 | tf_op jit(solution)/shard_map/ppermute | solution.py:28
  31.1 0.0 collective-permute-done.8.far_ref
  31.1 0.1 collective-permute-start.9
  31.2 1.1 %collective-permute-done.9.refs_5_ = f32[2,128]{1,0:T(2,128)S(1)} collective-permute-done((f32[2,128]{1,0:T(2,128)S(1)}, f32[2,128]{1,0:T(2,128)S(1)}, u32[]{:S(2)}, u32[]{:S(2)}) %collective-permute-start.9) | collective-permute-done | bytes 1056 | tf_op jit(solution)/shard_map/ppermute | solution.py:28
  32.2 0.0 collective-permute-done.7.refs_3_
  32.2 0.0 collective-permute-done.6.refs_2_
  32.3 0.6 %finish.1 = (f32[1,36]{1,0:T(1,128)}, f32[1,6]{1,0:T(1,128)}, f32[8,36]{1,0:T(8,128)}) custom-call(f32[4,128]{1,0:T(4,128)S(1)} %collective-permute-done.3.refs_0_, f32[4,128]{1,0:T(4,128)S(1)} %collective-permute-done.5.refs_1_, f32[4,128]{1,0:T(4,128)S(1)} %collective-permute-done.6.refs_2_, f32[4,128]{1,0:T(4,128)S(1)} %collective-permute-done.7.refs_3_, ...), custom_call_target="tpu_custom_call" | custom-call | tf_op jit(solution)/shard_map/finish/pallas_call | solution.py:239
  (3 shorter events, 0.0 us)
Async XLA Ops:
  1.7 17.2 %collective-permute-start = (f32[6,64,128]{2,1,0:T(8,128)S(1)}, f32[6,64,128]{2,1,0:T(8,128)S(1)}, u32[]{:S(2)}, u32[]{:S(2)}) collective-permute-start(f32[6,64,128]{2,1,0:T(8,128)S(1)} %get-tuple-element.17.table_ref), channel_id=1, source_target_pairs={{0,8},{1,9},{2,10},{3,11},{4,12},{5,13},{6,14},{7,15},{8,16},{9,17... | collective-permute-start | bytes 589832 | tf_op jit(solution)/shard_map/ppermute | solution.py:24
  3.8 2.2 %collective-permute-start.1 = (f32[2,2,4,8,128]{4,3,2,1,0:T(8,128)S(1)}, f32[2,2,4,8,128]{4,3,2,1,0:T(8,128)S(1)}, u32[]{:S(2)}, u32[]{:S(2)}) collective-permute-start(f32[2,2,4,8,128]{4,3,2,1,0:T(8,128)S(1)} %get-tuple-element.19), channel_id=1, source_target_pairs={{0,1},{1,0},{2,3},{3,2},{4,5},{5,4},{6,7},{7,6},{8,9},{9,8},{10,11... | collective-permute-start | bytes 196616 | tf_op jit(solution)/shard_map/ppermute | solution.py:28
  6.0 10.1 %collective-permute-start.2 = (f32[2,4,16,128]{3,2,1,0:T(8,128)S(1)}, f32[2,4,16,128]{3,2,1,0:T(8,128)S(1)}, u32[]{:S(2)}, u32[]{:S(2)}) collective-permute-start(f32[2,4,16,128]{3,2,1,0:T(8,128)S(1)} %get-tuple-element.20), channel_id=1, source_target_pairs={{0,248},{1,253},{2,250},{3,255},{4,252},{5,1},{6,254},{7,3},{8,0},... | collective-permute-start | bytes 196616 | tf_op jit(solution)/shard_map/ppermute | solution.py:24
  14.8 3.1 %collective-permute-start.4 = (f32[2,4,16,128]{3,2,1,0:T(8,128)S(1)}, f32[2,4,16,128]{3,2,1,0:T(8,128)S(1)}, u32[]{:S(2)}, u32[]{:S(2)}) collective-permute-start(f32[2,4,16,128]{3,2,1,0:T(8,128)S(1)} %get-tuple-element.22), channel_id=1, source_target_pairs={{0,250},{1,255},{2,252},{3,1},{4,254},{5,3},{6,0},{7,5},{8,2},{9,7... | collective-permute-start | bytes 196616 | tf_op jit(solution)/shard_map/ppermute | solution.py:24
  21.0 8.1 %collective-permute-start.5 = (f32[4,128]{1,0:T(4,128)S(1)}, f32[4,128]{1,0:T(4,128)S(1)}, u32[]{:S(2)}, u32[]{:S(2)}) collective-permute-start(f32[4,128]{1,0:T(4,128)S(1)} %get-tuple-element.24), channel_id=1, source_target_pairs={{0,6},{1,3},{2,8},{3,5},{4,10},{5,7},{6,12},{7,9},{8,14},{9,11},{1... | collective-permute-start | bytes 6152 | tf_op jit(solution)/shard_map/ppermute | solution.py:24
  21.8 8.2 %collective-permute-start.3 = (f32[4,128]{1,0:T(4,128)S(1)}, f32[4,128]{1,0:T(4,128)S(1)}, u32[]{:S(2)}, u32[]{:S(2)}) collective-permute-start(f32[4,128]{1,0:T(4,128)S(1)} %get-tuple-element.21), channel_id=1, source_target_pairs={{0,8},{1,5},{2,10},{3,7},{4,12},{5,9},{6,14},{7,11},{8,16},{9,13},... | collective-permute-start | bytes 6152 | tf_op jit(solution)/shard_map/ppermute | solution.py:24
  21.8 9.3 %collective-permute-start.8 = (f32[2,128]{1,0:T(2,128)S(1)}, f32[2,128]{1,0:T(2,128)S(1)}, u32[]{:S(2)}, u32[]{:S(2)}) collective-permute-start(f32[2,128]{1,0:T(2,128)S(1)} %get-tuple-element.27), channel_id=1, source_target_pairs={{0,248},{1,249},{2,250},{3,251},{4,252},{5,253},{6,254},{7,255},{8... | collective-permute-start | bytes 3080 | tf_op jit(solution)/shard_map/ppermute | solution.py:24
  29.2 3.1 %collective-permute-start.7 = (f32[4,128]{1,0:T(4,128)S(1)}, f32[4,128]{1,0:T(4,128)S(1)}, u32[]{:S(2)}, u32[]{:S(2)}) collective-permute-start(f32[4,128]{1,0:T(4,128)S(1)} %collective-permute-done.5.refs_1_), channel_id=1, source_target_pairs={{0,1},{1,0},{2,3},{3,2},{4,5},{5,4},{6,7},{7,6},{8,9},{9,8},{10,11... | collective-permute-start | bytes 6152 | tf_op jit(solution)/shard_map/ppermute | solution.py:28
  30.0 2.3 %collective-permute-start.6 = (f32[4,128]{1,0:T(4,128)S(1)}, f32[4,128]{1,0:T(4,128)S(1)}, u32[]{:S(2)}, u32[]{:S(2)}) collective-permute-start(f32[4,128]{1,0:T(4,128)S(1)} %collective-permute-done.3.refs_0_), channel_id=1, source_target_pairs={{0,1},{1,0},{2,3},{3,2},{4,5},{5,4},{6,7},{7,6},{8,9},{9,8},{10,11... | collective-permute-start | bytes 6152 | tf_op jit(solution)/shard_map/ppermute | solution.py:28
  31.1 1.2 %collective-permute-start.9 = (f32[2,128]{1,0:T(2,128)S(1)}, f32[2,128]{1,0:T(2,128)S(1)}, u32[]{:S(2)}, u32[]{:S(2)}) collective-permute-start(f32[2,128]{1,0:T(2,128)S(1)} %join.1.refs_4_), channel_id=1, source_target_pairs={{0,1},{1,0},{2,3},{3,2},{4,5},{5,4},{6,7},{7,6},{8,9},{9,8},{10,11... | collective-permute-start | bytes 3080 | tf_op jit(solution)/shard_map/ppermute | solution.py:28

commit v4 on v3

--- a/solution.py
+++ b/solution.py
@@ -19,8 +19,8 @@
 SMEM = pl.BlockSpec(memory_space=pltpu.SMEM)
 
 
-def routed(block, blk, shifts):
-    route = [(i * 2 + r, (i + shifts[r]) % blk * 2 + r) for i in range(blk) for r in range(2)]
+def routed(block, blk, shifts, cross=False):
+    route = [(i * 2 + r, (i + shifts[r]) % blk * 2 + (1 - r if cross else r)) for i in range(blk) for r in range(2)]
     return lax.ppermute(block, ("blk", "rep"), route)
 
 
@@ -49,7 +49,7 @@
 
 
 def step_of(m, rep):
-    return 3 - m - 2 * rep
+    return 3 - rep if m else rep
 
 
 def pack_kernel(src_ref, active_ref, points_ref, normals_ref, index_ref, table_ref, *outs):
@@ -224,6 +224,8 @@
         )(*map(near, (far_table, message, sums, *totals)))
         totals = [last]
         back.append(routed(rows, blk, step))
+    crossed = routed(rows, blk, steps[1], cross=True)
+    others = [swapped(back[0]), crossed]
     total = pltpu.VMEM((2, LANES), f32)
     here_total, far_total = pl.pallas_call(
         split_kernel, in_specs=[VMEM], out_specs=[VMEM] * 2, out_shape=[total] * 2, name="split"
@@ -233,9 +235,6 @@
         join_kernel, in_specs=[VMEM] * 2, out_specs=VMEM, out_shape=total, name="join"
     )(near(here_total), near(far_total))
     other_total = swapped(total)
-    others = []
-    for x in back:
-        others.append(swapped(x))
     diag, grad, pairs = pl.pallas_call(
         functools.partial(finish_kernel, scale=1.0 / (2.0 * rounds)),
         in_specs=[VMEM] * 6,

time: 33 us -> 36.2 us (1.097)
  waiting for transfers between devices: 3.78 us -> 6.09 us
  starting transfers between devices: 22.6 us -> 23.5 us
    ppermute x6 -> x7, waiting for transfers between devices: 1.8 us -> 4.36 us  [routed(): return lax.ppermute(block, ('blk', 'rep'), route)]
    ppermute x6 -> x7, starting transfers between devices: 19.8 us -> 21.7 us  [routed(): return lax.ppermute(block, ('blk', 'rep'), route)]
    ppermute x4 -> x3, starting transfers between devices: 2.85 us -> 1.77 us  [swapped(): return lax.ppermute(block, 'rep', [(0, 1), (1, 0)])]
    ppermute x4 -> x3, waiting for transfers between devices: 1.98 us -> 1.72 us  [swapped(): return lax.ppermute(block, 'rep', [(0, 1), (1, 0)])]
  transfers between devices with their start and end apart: 10 -> 10, of which waited for: 5 -> 4; matrix products, arithmetic and copies ran while one was open for 0% -> 0% of each run, Pallas kernels for 6% -> 11%
where the time goes in v4:
time: 36.2 us; the launch traced here: 36.1 us
  starting transfers between devices  23.5 us (65%)
  waiting for transfers between devices  6.09 us (17%)
  Pallas kernels  5.78 us (16%)
  between operations  0.71 us (2%)
    ppermute x7, starting transfers between devices, routed(): return lax.ppermute(block, ('blk', 'rep'), route)  21.7 us
    ppermute x7, waiting for transfers between devices, routed(): return lax.ppermute(block, ('blk', 'rep'), route)  4.36 us
    pallas_call x2, Pallas kernels, body(): pl.pallas_call(far_kernel, in_specs=[VMEM] * (3 + len(totals)), out_specs...  2.12 us
    pallas_call x2, Pallas kernels, body(): pl.pallas_call(near_kernel, in_specs=[VMEM] * 2, out_specs=VMEM, out_shap...  1.95 us
    ppermute x3, starting transfers between devices, swapped(): return lax.ppermute(block, 'rep', [(0, 1), (1, 0)])  1.77 us
    ppermute x3, waiting for transfers between devices, swapped(): return lax.ppermute(block, 'rep', [(0, 1), (1, 0)])  1.72 us
    pallas_call x1, Pallas kernels, body(): pl.pallas_call(pack_kernel, in_specs=[SMEM, SMEM, VMEM, VMEM, VMEM], out_...  1.08 us
  transfers between devices with their start and end apart: 10, of which 4 were waited for; matrix products, arithmetic and copies ran while one was open for 0% of the time, Pallas kernels for 11%

profile of v4, /device:TPU:1, one launch (start us, length us, event | category | flops | bytes accessed | tf_op | source)
XLA Modules:
  0.0 36.1 jit_solution(781877334926723812)
XLA Ops:
  0.6 1.1 %pack.1 = (f32[6,64,128]{2,1,0:T(8,128)S(1)}, f32[2,2,4,8,128]{4,3,2,1,0:T(8,128)S(1)}, f32[2,2,4,8,128]{4,3,2,1,0:T(8,128)S(1)}) custom-call(s32[8,8]{1,0:T(8,128)} %bitcast.11, s32[1,8]{1,0:T(1,128)} %bitcast.12, f32[3,64,128]{2,1,0:T(8,128)} %bitcast.8, f32[3,64,128]{2,1,0:T(8,128)} %bitcast.9, s32[8,8,128]{2,1,0:T(8,128)} %bitcast.10), custom_call_target="tpu_custom_call" | custom-call | tf_op jit(solution)/shard_map/pack/pallas_call | solution.py:183
  1.7 2.1 %collective-permute-start = (f32[6,64,128]{2,1,0:T(8,128)S(1)}, f32[6,64,128]{2,1,0:T(8,128)S(1)}, u32[]{:S(2)}, u32[]{:S(2)}) collective-permute-start(f32[6,64,128]{2,1,0:T(8,128)S(1)} %get-tuple-element.17.table_ref), channel_id=1, source_target_pairs={{0,8},{1,9},{2,10},{3,11},{4,12},{5,13},{6,14},{7,15},{8,16},{9,17... | collective-permute-start | bytes 589832 | tf_op jit(solution)/shard_map/ppermute | solution.py:24
  3.8 1.3 %collective-permute-start.1 = (f32[2,2,4,8,128]{4,3,2,1,0:T(8,128)S(1)}, f32[2,2,4,8,128]{4,3,2,1,0:T(8,128)S(1)}, u32[]{:S(2)}, u32[]{:S(2)}) collective-permute-start(f32[2,2,4,8,128]{4,3,2,1,0:T(8,128)S(1)} %get-tuple-element.19), channel_id=1, source_target_pairs={{0,1},{1,0},{2,3},{3,2},{4,5},{5,4},{6,7},{7,6},{8,9},{9,8},{10,11... | collective-permute-start | bytes 196616 | tf_op jit(solution)/shard_map/ppermute | solution.py:28
  5.1 0.9 %collective-permute-done.1.other_ref = f32[2,2,4,8,128]{4,3,2,1,0:T(8,128)S(1)} collective-permute-done((f32[2,2,4,8,128]{4,3,2,1,0:T(8,128)S(1)}, f32[2,2,4,8,128]{4,3,2,1,0:T(8,128)S(1)}, u32[]{:S(2)}, u32[]{:S(2)}) %collective-permute-start.1) | collective-permute-done | bytes 65568 | tf_op jit(solution)/shard_map/ppermute | solution.py:28
  6.0 8.8 %collective-permute-start.2 = (f32[2,4,16,128]{3,2,1,0:T(8,128)S(1)}, f32[2,4,16,128]{3,2,1,0:T(8,128)S(1)}, u32[]{:S(2)}, u32[]{:S(2)}) collective-permute-start(f32[2,4,16,128]{3,2,1,0:T(8,128)S(1)} %get-tuple-element.20), channel_id=1, source_target_pairs={{0,254},{1,253},{2,0},{3,255},{4,2},{5,1},{6,4},{7,3},{8,6},{9,5},... | collective-permute-start | bytes 196616 | tf_op jit(solution)/shard_map/ppermute | solution.py:24
  14.8 1.8 %collective-permute-start.4 = (f32[2,4,16,128]{3,2,1,0:T(8,128)S(1)}, f32[2,4,16,128]{3,2,1,0:T(8,128)S(1)}, u32[]{:S(2)}, u32[]{:S(2)}) collective-permute-start(f32[2,4,16,128]{3,2,1,0:T(8,128)S(1)} %get-tuple-element.22), channel_id=1, source_target_pairs={{0,248},{1,251},{2,250},{3,253},{4,252},{5,255},{6,254},{7,1},{8,0... | collective-permute-start | bytes 196616 | tf_op jit(solution)/shard_map/ppermute | solution.py:24
  16.5 0.0 collective-permute-done.2.message_ref
  16.5 1.0 %near.2.near_ref = f32[32,128]{1,0:T(8,128)S(1)} custom-call(f32[6,64,128]{2,1,0:T(8,128)S(1)} %get-tuple-element.17.table_ref, f32[2,4,16,128]{3,2,1,0:T(8,128)S(1)} %collective-permute-done.2.message_ref), custom_call_target="tpu_custom_call" | custom-call | tf_op jit(solution)/shard_map/near/pallas_call | solution.py:210
  17.5 0.0 collective-permute-done.table_ref
  17.5 1.1 %far.2 = (f32[4,128]{1,0:T(4,128)S(1)}, f32[4,128]{1,0:T(4,128)S(1)}) custom-call(f32[6,64,128]{2,1,0:T(8,128)S(1)} %collective-permute-done.table_ref, f32[2,4,16,128]{3,2,1,0:T(8,128)S(1)} %collective-permute-done.2.message_ref, f32[32,128]{1,0:T(8,128)S(1)} %near.2.near_ref), custom_call_target="tpu_custom_call" | custom-call | tf_op jit(solution)/shard_map/far/pallas_call | solution.py:217
  18.6 0.4 %collective-permute-start.3 = (f32[4,128]{1,0:T(4,128)S(1)}, f32[4,128]{1,0:T(4,128)S(1)}, u32[]{:S(2)}, u32[]{:S(2)}) collective-permute-start(f32[4,128]{1,0:T(4,128)S(1)} %get-tuple-element.21), channel_id=1, source_target_pairs={{0,2},{1,5},{2,4},{3,7},{4,6},{5,9},{6,8},{7,11},{8,10},{9,13},{10... | collective-permute-start | bytes 6152 | tf_op jit(solution)/shard_map/ppermute | solution.py:24
  19.0 0.1 collective-permute-done.4.message_ref
  19.1 1.0 %near.3.near_ref = f32[32,128]{1,0:T(8,128)S(1)} custom-call(f32[6,64,128]{2,1,0:T(8,128)S(1)} %get-tuple-element.17.table_ref, f32[2,4,16,128]{3,2,1,0:T(8,128)S(1)} %collective-permute-done.4.message_ref), custom_call_target="tpu_custom_call" | custom-call | tf_op jit(solution)/shard_map/near/pallas_call | solution.py:210
  20.1 1.1 %far.3 = (f32[4,128]{1,0:T(4,128)S(1)}, f32[4,128]{1,0:T(4,128)S(1)}) custom-call(f32[6,64,128]{2,1,0:T(8,128)S(1)} %collective-permute-done.table_ref, f32[2,4,16,128]{3,2,1,0:T(8,128)S(1)} %collective-permute-done.4.message_ref, f32[32,128]{1,0:T(8,128)S(1)} %near.3.near_ref, f32[4,128]{1,0:T(4,128)S(1)} %get-tuple-element.23.refs_0_), custom_call_target="tpu_custom_call" | custom-call | tf_op jit(solution)/shard_map/far/pallas_call | solution.py:217
  21.2 7.6 %collective-permute-start.8 = (f32[2,128]{1,0:T(2,128)S(1)}, f32[2,128]{1,0:T(2,128)S(1)}, u32[]{:S(2)}, u32[]{:S(2)}) collective-permute-start(f32[2,128]{1,0:T(2,128)S(1)} %get-tuple-element.27), channel_id=1, source_target_pairs={{0,248},{1,249},{2,250},{3,251},{4,252},{5,253},{6,254},{7,255},{8... | collective-permute-start | bytes 3080 | tf_op jit(solution)/shard_map/ppermute | solution.py:24
  28.8 0.0 collective-permute-start.5
  28.8 1.0 %collective-permute-start.7 = (f32[4,128]{1,0:T(4,128)S(1)}, f32[4,128]{1,0:T(4,128)S(1)}, u32[]{:S(2)}, u32[]{:S(2)}) collective-permute-start(f32[4,128]{1,0:T(4,128)S(1)} %get-tuple-element.24), channel_id=1, source_target_pairs={{0,9},{1,6},{2,11},{3,8},{4,13},{5,10},{6,15},{7,12},{8,17},{9,14}... | collective-permute-start | bytes 6152 | tf_op jit(solution)/shard_map/ppermute | solution.py:24
  29.8 0.0 collective-permute-done.3.refs_0_
  29.8 0.0 collective-permute-start.6
  29.8 0.0 collective-permute-done.8.far_ref
  29.8 0.5 %collective-permute-start.9 = (f32[2,128]{1,0:T(2,128)S(1)}, f32[2,128]{1,0:T(2,128)S(1)}, u32[]{:S(2)}, u32[]{:S(2)}) collective-permute-start(f32[2,128]{1,0:T(2,128)S(1)} %join.1.refs_4_), channel_id=1, source_target_pairs={{0,1},{1,0},{2,3},{3,2},{4,5},{5,4},{6,7},{7,6},{8,9},{9,8},{10,11... | collective-permute-start | bytes 3080 | tf_op jit(solution)/shard_map/ppermute | solution.py:28
  30.3 0.8 %collective-permute-done.9.refs_5_ = f32[2,128]{1,0:T(2,128)S(1)} collective-permute-done((f32[2,128]{1,0:T(2,128)S(1)}, f32[2,128]{1,0:T(2,128)S(1)}, u32[]{:S(2)}, u32[]{:S(2)}) %collective-permute-start.9) | collective-permute-done | bytes 1056 | tf_op jit(solution)/shard_map/ppermute | solution.py:28
  31.2 4.3 %collective-permute-done.5.refs_1_ = f32[4,128]{1,0:T(4,128)S(1)} collective-permute-done((f32[4,128]{1,0:T(4,128)S(1)}, f32[4,128]{1,0:T(4,128)S(1)}, u32[]{:S(2)}, u32[]{:S(2)}) %collective-permute-start.5) | collective-permute-done | bytes 2080 | tf_op jit(solution)/shard_map/ppermute | solution.py:24
  35.5 0.0 collective-permute-done.7.refs_3_
  35.5 0.0 collective-permute-done.6.refs_2_
  35.5 0.6 %finish.1 = (f32[1,36]{1,0:T(1,128)}, f32[1,6]{1,0:T(1,128)}, f32[8,36]{1,0:T(8,128)}) custom-call(f32[4,128]{1,0:T(4,128)S(1)} %collective-permute-done.3.refs_0_, f32[4,128]{1,0:T(4,128)S(1)} %collective-permute-done.5.refs_1_, f32[4,128]{1,0:T(4,128)S(1)} %collective-permute-done.6.refs_2_, f32[4,128]{1,0:T(4,128)S(1)} %collective-permute-done.7.refs_3_, ...), custom_call_target="tpu_custom_call" | custom-call | tf_op jit(solution)/shard_map/finish/pallas_call | solution.py:238
  (3 shorter events, 0.0 us)
Async XLA Ops:
  1.7 15.8 %collective-permute-start = (f32[6,64,128]{2,1,0:T(8,128)S(1)}, f32[6,64,128]{2,1,0:T(8,128)S(1)}, u32[]{:S(2)}, u32[]{:S(2)}) collective-permute-start(f32[6,64,128]{2,1,0:T(8,128)S(1)} %get-tuple-element.17.table_ref), channel_id=1, source_target_pairs={{0,8},{1,9},{2,10},{3,11},{4,12},{5,13},{6,14},{7,15},{8,16},{9,17... | collective-permute-start | bytes 589832 | tf_op jit(solution)/shard_map/ppermute | solution.py:24
  3.8 2.2 %collective-permute-start.1 = (f32[2,2,4,8,128]{4,3,2,1,0:T(8,128)S(1)}, f32[2,2,4,8,128]{4,3,2,1,0:T(8,128)S(1)}, u32[]{:S(2)}, u32[]{:S(2)}) collective-permute-start(f32[2,2,4,8,128]{4,3,2,1,0:T(8,128)S(1)} %get-tuple-element.19), channel_id=1, source_target_pairs={{0,1},{1,0},{2,3},{3,2},{4,5},{5,4},{6,7},{7,6},{8,9},{9,8},{10,11... | collective-permute-start | bytes 196616 | tf_op jit(solution)/shard_map/ppermute | solution.py:28
  6.0 10.5 %collective-permute-start.2 = (f32[2,4,16,128]{3,2,1,0:T(8,128)S(1)}, f32[2,4,16,128]{3,2,1,0:T(8,128)S(1)}, u32[]{:S(2)}, u32[]{:S(2)}) collective-permute-start(f32[2,4,16,128]{3,2,1,0:T(8,128)S(1)} %get-tuple-element.20), channel_id=1, source_target_pairs={{0,254},{1,253},{2,0},{3,255},{4,2},{5,1},{6,4},{7,3},{8,6},{9,5},... | collective-permute-start | bytes 196616 | tf_op jit(solution)/shard_map/ppermute | solution.py:24
  14.8 4.3 %collective-permute-start.4 = (f32[2,4,16,128]{3,2,1,0:T(8,128)S(1)}, f32[2,4,16,128]{3,2,1,0:T(8,128)S(1)}, u32[]{:S(2)}, u32[]{:S(2)}) collective-permute-start(f32[2,4,16,128]{3,2,1,0:T(8,128)S(1)} %get-tuple-element.22), channel_id=1, source_target_pairs={{0,248},{1,251},{2,250},{3,253},{4,252},{5,255},{6,254},{7,1},{8,0... | collective-permute-start | bytes 196616 | tf_op jit(solution)/shard_map/ppermute | solution.py:24
  18.6 11.2 %collective-permute-start.3 = (f32[4,128]{1,0:T(4,128)S(1)}, f32[4,128]{1,0:T(4,128)S(1)}, u32[]{:S(2)}, u32[]{:S(2)}) collective-permute-start(f32[4,128]{1,0:T(4,128)S(1)} %get-tuple-element.21), channel_id=1, source_target_pairs={{0,2},{1,5},{2,4},{3,7},{4,6},{5,9},{6,8},{7,11},{8,10},{9,13},{10... | collective-permute-start | bytes 6152 | tf_op jit(solution)/shard_map/ppermute | solution.py:24
  21.2 8.7 %collective-permute-start.8 = (f32[2,128]{1,0:T(2,128)S(1)}, f32[2,128]{1,0:T(2,128)S(1)}, u32[]{:S(2)}, u32[]{:S(2)}) collective-permute-start(f32[2,128]{1,0:T(2,128)S(1)} %get-tuple-element.27), channel_id=1, source_target_pairs={{0,248},{1,249},{2,250},{3,251},{4,252},{5,253},{6,254},{7,255},{8... | collective-permute-start | bytes 3080 | tf_op jit(solution)/shard_map/ppermute | solution.py:24
  28.8 6.7 %collective-permute-start.5 = (f32[4,128]{1,0:T(4,128)S(1)}, f32[4,128]{1,0:T(4,128)S(1)}, u32[]{:S(2)}, u32[]{:S(2)}) collective-permute-start(f32[4,128]{1,0:T(4,128)S(1)} %get-tuple-element.24), channel_id=1, source_target_pairs={{0,8},{1,7},{2,10},{3,9},{4,12},{5,11},{6,14},{7,13},{8,16},{9,15}... | collective-permute-start | bytes 6152 | tf_op jit(solution)/shard_map/ppermute | solution.py:24
  28.8 6.7 %collective-permute-start.7 = (f32[4,128]{1,0:T(4,128)S(1)}, f32[4,128]{1,0:T(4,128)S(1)}, u32[]{:S(2)}, u32[]{:S(2)}) collective-permute-start(f32[4,128]{1,0:T(4,128)S(1)} %get-tuple-element.24), channel_id=1, source_target_pairs={{0,9},{1,6},{2,11},{3,8},{4,13},{5,10},{6,15},{7,12},{8,17},{9,14}... | collective-permute-start | bytes 6152 | tf_op jit(solution)/shard_map/ppermute | solution.py:24
  29.8 5.6 %collective-permute-start.6 = (f32[4,128]{1,0:T(4,128)S(1)}, f32[4,128]{1,0:T(4,128)S(1)}, u32[]{:S(2)}, u32[]{:S(2)}) collective-permute-start(f32[4,128]{1,0:T(4,128)S(1)} %collective-permute-done.3.refs_0_), channel_id=1, source_target_pairs={{0,1},{1,0},{2,3},{3,2},{4,5},{5,4},{6,7},{7,6},{8,9},{9,8},{10,11... | collective-permute-start | bytes 6152 | tf_op jit(solution)/shard_map/ppermute | solution.py:28
  29.8 1.3 %collective-permute-start.9 = (f32[2,128]{1,0:T(2,128)S(1)}, f32[2,128]{1,0:T(2,128)S(1)}, u32[]{:S(2)}, u32[]{:S(2)}) collective-permute-start(f32[2,128]{1,0:T(2,128)S(1)} %join.1.refs_4_), channel_id=1, source_target_pairs={{0,1},{1,0},{2,3},{3,2},{4,5},{5,4},{6,7},{7,6},{8,9},{9,8},{10,11... | collective-permute-start | bytes 3080 | tf_op jit(solution)/shard_map/ppermute | solution.py:28

commit v5 on v4

--- a/solution.py
+++ b/solution.py
@@ -49,7 +49,7 @@
 
 
 def step_of(m, rep):
-    return 3 - rep if m else rep
+    return rep if m else 3 - rep
 
 
 def pack_kernel(src_ref, active_ref, points_ref, normals_ref, index_ref, table_ref, *outs):
@@ -151,13 +151,9 @@
         totals_ref[at + 1 : at + 2, :] = push
 
 
-def split_kernel(totals_ref, here_ref, far_ref):
-    here_ref[...] = totals_ref[0:2, :]
-    far_ref[...] = totals_ref[2:4, :]
-
-
-def join_kernel(here_ref, far_ref, total_ref):
-    total_ref[...] = here_ref[...] + far_ref[...]
+def join_kernel(own_ref, other_ref, here_ref, far_ref):
+    here_ref[...] = own_ref[0:2, :] + other_ref[0:2, :]
+    far_ref[...] = own_ref[2:4, :] + other_ref[2:4, :]
 
 
 def finish_kernel(*refs, scale):
@@ -226,15 +222,15 @@
         back.append(routed(rows, blk, step))
     crossed = routed(rows, blk, steps[1], cross=True)
     others = [swapped(back[0]), crossed]
-    total = pltpu.VMEM((2, LANES), f32)
+    other_total = swapped(totals[0])
     here_total, far_total = pl.pallas_call(
-        split_kernel, in_specs=[VMEM], out_specs=[VMEM] * 2, out_shape=[total] * 2, name="split"
-    )(near(totals[0]))
+        join_kernel,
+        in_specs=[VMEM] * 2,
+        out_specs=[VMEM] * 2,
+        out_shape=[pltpu.VMEM((2, LANES), f32)] * 2,
+        name="join",
+    )(near(totals[0]), near(other_total))
     far_total = routed(far_total, blk, (-FAR, -FAR))
-    total = pl.pallas_call(
-        join_kernel, in_specs=[VMEM] * 2, out_specs=VMEM, out_shape=total, name="join"
-    )(near(here_total), near(far_total))
-    other_total = swapped(total)
     diag, grad, pairs = pl.pallas_call(
         functools.partial(finish_kernel, scale=1.0 / (2.0 * rounds)),
         in_specs=[VMEM] * 6,
@@ -245,7 +241,7 @@
             jax.ShapeDtypeStruct((rounds, 36), f32),
         ],
         name="finish",
-    )(*(near(x) for x in (*back, *others, total, other_total)))
+    )(*(near(x) for x in (*back, *others, here_total, far_total)))
     return diag, grad, pairs.reshape(rounds, 1, 1, 36)
 
 

time: 36.2 us -> 33.2 us (0.917)
  waiting for transfers between devices: 6.09 us -> 2.35 us
  starting transfers between devices: 23.5 us -> 24.3 us
    ppermute x7, waiting for transfers between devices: 4.36 us -> 1.45 us  [routed(): return lax.ppermute(block, ('blk', 'rep'), route)]
    ppermute x3, waiting for transfers between devices: 1.72 us -> 0.91 us  [swapped(): return lax.ppermute(block, 'rep', [(0, 1), (1, 0)])]
    ppermute x7, starting transfers between devices: 21.7 us -> 22.5 us  [routed(): return lax.ppermute(block, ('blk', 'rep'), route)]
  transfers between devices with their start and end apart: 10 -> 10, of which waited for: 4 -> 2; matrix products, arithmetic and copies ran while one was open for 0% -> 0% of each run, Pallas kernels for 11% -> 12%
where the time goes in v5:
time: 33.2 us; the launch traced here: 33.1 us
  starting transfers between devices  24.3 us (73%)
  Pallas kernels  5.78 us (17%)
  waiting for transfers between devices  2.35 us (7%)
  between operations  0.7 us (2%)
    ppermute x7, starting transfers between devices, routed(): return lax.ppermute(block, ('blk', 'rep'), route)  22.5 us
    pallas_call x2, Pallas kernels, body(): pl.pallas_call(far_kernel, in_specs=[VMEM] * (3 + len(totals)), out_specs...  2.12 us
    pallas_call x2, Pallas kernels, body(): pl.pallas_call(near_kernel, in_specs=[VMEM] * 2, out_specs=VMEM, out_shap...  1.95 us
    ppermute x3, starting transfers between devices, swapped(): return lax.ppermute(block, 'rep', [(0, 1), (1, 0)])  1.72 us
    ppermute x7, waiting for transfers between devices, routed(): return lax.ppermute(block, ('blk', 'rep'), route)  1.45 us
    pallas_call x1, Pallas kernels, body(): pl.pallas_call(pack_kernel, in_specs=[SMEM, SMEM, VMEM, VMEM, VMEM], out_...  1.08 us
    ppermute x3, waiting for transfers between devices, swapped(): return lax.ppermute(block, 'rep', [(0, 1), (1, 0)])  0.91 us
  transfers between devices with their start and end apart: 10, of which 2 were waited for; matrix products, arithmetic and copies ran while one was open for 0% of the time, Pallas kernels for 12%

profile of v5, /device:TPU:1, one launch (start us, length us, event | category | flops | bytes accessed | tf_op | source)
XLA Modules:
  0.0 33.1 jit_solution(2133618503574366422)
XLA Ops:
  0.6 1.1 %pack.1 = (f32[6,64,128]{2,1,0:T(8,128)S(1)}, f32[2,2,4,8,128]{4,3,2,1,0:T(8,128)S(1)}, f32[2,2,4,8,128]{4,3,2,1,0:T(8,128)S(1)}) custom-call(s32[8,8]{1,0:T(8,128)} %bitcast.11, s32[1,8]{1,0:T(1,128)} %bitcast.12, f32[3,64,128]{2,1,0:T(8,128)} %bitcast.8, f32[3,64,128]{2,1,0:T(8,128)} %bitcast.9, s32[8,8,128]{2,1,0:T(8,128)} %bitcast.10), custom_call_target="tpu_custom_call" | custom-call | tf_op jit(solution)/shard_map/pack/pallas_call | solution.py:179
  1.7 2.1 %collective-permute-start = (f32[6,64,128]{2,1,0:T(8,128)S(1)}, f32[6,64,128]{2,1,0:T(8,128)S(1)}, u32[]{:S(2)}, u32[]{:S(2)}) collective-permute-start(f32[6,64,128]{2,1,0:T(8,128)S(1)} %get-tuple-element.17.table_ref), channel_id=1, source_target_pairs={{0,8},{1,9},{2,10},{3,11},{4,12},{5,13},{6,14},{7,15},{8,16},{9,17... | collective-permute-start | bytes 589832 | tf_op jit(solution)/shard_map/ppermute | solution.py:24
  3.8 1.3 %collective-permute-start.1 = (f32[2,2,4,8,128]{4,3,2,1,0:T(8,128)S(1)}, f32[2,2,4,8,128]{4,3,2,1,0:T(8,128)S(1)}, u32[]{:S(2)}, u32[]{:S(2)}) collective-permute-start(f32[2,2,4,8,128]{4,3,2,1,0:T(8,128)S(1)} %get-tuple-element.19), channel_id=1, source_target_pairs={{0,1},{1,0},{2,3},{3,2},{4,5},{5,4},{6,7},{7,6},{8,9},{9,8},{10,11... | collective-permute-start | bytes 196616 | tf_op jit(solution)/shard_map/ppermute | solution.py:28
  5.1 0.9 %collective-permute-done.1.other_ref = f32[2,2,4,8,128]{4,3,2,1,0:T(8,128)S(1)} collective-permute-done((f32[2,2,4,8,128]{4,3,2,1,0:T(8,128)S(1)}, f32[2,2,4,8,128]{4,3,2,1,0:T(8,128)S(1)}, u32[]{:S(2)}, u32[]{:S(2)}) %collective-permute-start.1) | collective-permute-done | bytes 65568 | tf_op jit(solution)/shard_map/ppermute | solution.py:28
  6.0 7.1 %collective-permute-start.2 = (f32[2,4,16,128]{3,2,1,0:T(8,128)S(1)}, f32[2,4,16,128]{3,2,1,0:T(8,128)S(1)}, u32[]{:S(2)}, u32[]{:S(2)}) collective-permute-start(f32[2,4,16,128]{3,2,1,0:T(8,128)S(1)} %get-tuple-element.20), channel_id=1, source_target_pairs={{0,248},{1,251},{2,250},{3,253},{4,252},{5,255},{6,254},{7,1},{8,0... | collective-permute-start | bytes 196616 | tf_op jit(solution)/shard_map/ppermute | solution.py:24
  13.2 4.0 %collective-permute-start.4 = (f32[2,4,16,128]{3,2,1,0:T(8,128)S(1)}, f32[2,4,16,128]{3,2,1,0:T(8,128)S(1)}, u32[]{:S(2)}, u32[]{:S(2)}) collective-permute-start(f32[2,4,16,128]{3,2,1,0:T(8,128)S(1)} %get-tuple-element.22), channel_id=1, source_target_pairs={{0,254},{1,253},{2,0},{3,255},{4,2},{5,1},{6,4},{7,3},{8,6},{9,5},... | collective-permute-start | bytes 196616 | tf_op jit(solution)/shard_map/ppermute | solution.py:24
  17.1 0.0 collective-permute-done.2.message_ref
  17.1 1.0 %near.2.near_ref = f32[32,128]{1,0:T(8,128)S(1)} custom-call(f32[6,64,128]{2,1,0:T(8,128)S(1)} %get-tuple-element.17.table_ref, f32[2,4,16,128]{3,2,1,0:T(8,128)S(1)} %collective-permute-done.2.message_ref), custom_call_target="tpu_custom_call" | custom-call | tf_op jit(solution)/shard_map/near/pallas_call | solution.py:206
  18.1 0.0 collective-permute-done.table_ref
  18.1 1.1 %far.2 = (f32[4,128]{1,0:T(4,128)S(1)}, f32[4,128]{1,0:T(4,128)S(1)}) custom-call(f32[6,64,128]{2,1,0:T(8,128)S(1)} %collective-permute-done.table_ref, f32[2,4,16,128]{3,2,1,0:T(8,128)S(1)} %collective-permute-done.2.message_ref, f32[32,128]{1,0:T(8,128)S(1)} %near.2.near_ref), custom_call_target="tpu_custom_call" | custom-call | tf_op jit(solution)/shard_map/far/pallas_call | solution.py:213
  19.2 0.1 collective-permute-start.3
  19.3 0.0 collective-permute-done.4.message_ref
  19.3 1.0 %near.3.near_ref = f32[32,128]{1,0:T(8,128)S(1)} custom-call(f32[6,64,128]{2,1,0:T(8,128)S(1)} %get-tuple-element.17.table_ref, f32[2,4,16,128]{3,2,1,0:T(8,128)S(1)} %collective-permute-done.4.message_ref), custom_call_target="tpu_custom_call" | custom-call | tf_op jit(solution)/shard_map/near/pallas_call | solution.py:206
  20.3 1.1 %far.3 = (f32[4,128]{1,0:T(4,128)S(1)}, f32[4,128]{1,0:T(4,128)S(1)}) custom-call(f32[6,64,128]{2,1,0:T(8,128)S(1)} %collective-permute-done.table_ref, f32[2,4,16,128]{3,2,1,0:T(8,128)S(1)} %collective-permute-done.4.message_ref, f32[32,128]{1,0:T(8,128)S(1)} %near.3.near_ref, f32[4,128]{1,0:T(4,128)S(1)} %get-tuple-element.23.refs_0_), custom_call_target="tpu_custom_call" | custom-call | tf_op jit(solution)/shard_map/far/pallas_call | solution.py:213
  21.4 0.2 collective-permute-start.8
  21.6 2.4 %collective-permute-start.5 = (f32[4,128]{1,0:T(4,128)S(1)}, f32[4,128]{1,0:T(4,128)S(1)}, u32[]{:S(2)}, u32[]{:S(2)}) collective-permute-start(f32[4,128]{1,0:T(4,128)S(1)} %get-tuple-element.24), channel_id=1, source_target_pairs={{0,2},{1,5},{2,4},{3,7},{4,6},{5,9},{6,8},{7,11},{8,10},{9,13},{10... | collective-permute-start | bytes 6152 | tf_op jit(solution)/shard_map/ppermute | solution.py:24
  24.0 1.9 %collective-permute-start.7 = (f32[4,128]{1,0:T(4,128)S(1)}, f32[4,128]{1,0:T(4,128)S(1)}, u32[]{:S(2)}, u32[]{:S(2)}) collective-permute-start(f32[4,128]{1,0:T(4,128)S(1)} %get-tuple-element.24), channel_id=1, source_target_pairs={{0,3},{1,4},{2,5},{3,6},{4,7},{5,8},{6,9},{7,10},{8,11},{9,12},{10... | collective-permute-start | bytes 6152 | tf_op jit(solution)/shard_map/ppermute | solution.py:24
  26.0 0.0 collective-permute-done.3.refs_0_
  26.0 0.2 collective-permute-start.6
  26.2 0.0 collective-permute-done.8.other_ref
  26.2 4.8 %collective-permute-start.9 = (f32[2,128]{1,0:T(2,128)S(1)}, f32[2,128]{1,0:T(2,128)S(1)}, u32[]{:S(2)}, u32[]{:S(2)}) collective-permute-start(f32[2,128]{1,0:T(2,128)S(1)} %get-tuple-element.27), channel_id=1, source_target_pairs={{0,248},{1,249},{2,250},{3,251},{4,252},{5,253},{6,254},{7,255},{8... | collective-permute-start | bytes 3080 | tf_op jit(solution)/shard_map/ppermute | solution.py:24
  31.0 0.0 collective-permute-done.5.refs_1_
  31.0 1.4 %collective-permute-done.7.refs_3_ = f32[4,128]{1,0:T(4,128)S(1)} collective-permute-done((f32[4,128]{1,0:T(4,128)S(1)}, f32[4,128]{1,0:T(4,128)S(1)}, u32[]{:S(2)}, u32[]{:S(2)}) %collective-permute-start.7) | collective-permute-done | bytes 2080 | tf_op jit(solution)/shard_map/ppermute | solution.py:24
  32.5 0.0 collective-permute-done.9.refs_5_
  32.5 0.0 collective-permute-done.6.refs_2_
  32.5 0.6 %finish.1 = (f32[1,36]{1,0:T(1,128)}, f32[1,6]{1,0:T(1,128)}, f32[8,36]{1,0:T(8,128)}) custom-call(f32[4,128]{1,0:T(4,128)S(1)} %collective-permute-done.3.refs_0_, f32[4,128]{1,0:T(4,128)S(1)} %collective-permute-done.5.refs_1_, f32[4,128]{1,0:T(4,128)S(1)} %collective-permute-done.6.refs_2_, f32[4,128]{1,0:T(4,128)S(1)} %collective-permute-done.7.refs_3_, ...), custom_call_target="tpu_custom_call" | custom-call | tf_op jit(solution)/shard_map/finish/pallas_call | solution.py:234
  (2 shorter events, 0.0 us)
Async XLA Ops:
  1.7 16.4 %collective-permute-start = (f32[6,64,128]{2,1,0:T(8,128)S(1)}, f32[6,64,128]{2,1,0:T(8,128)S(1)}, u32[]{:S(2)}, u32[]{:S(2)}) collective-permute-start(f32[6,64,128]{2,1,0:T(8,128)S(1)} %get-tuple-element.17.table_ref), channel_id=1, source_target_pairs={{0,8},{1,9},{2,10},{3,11},{4,12},{5,13},{6,14},{7,15},{8,16},{9,17... | collective-permute-start | bytes 589832 | tf_op jit(solution)/shard_map/ppermute | solution.py:24
  3.8 2.2 %collective-permute-start.1 = (f32[2,2,4,8,128]{4,3,2,1,0:T(8,128)S(1)}, f32[2,2,4,8,128]{4,3,2,1,0:T(8,128)S(1)}, u32[]{:S(2)}, u32[]{:S(2)}) collective-permute-start(f32[2,2,4,8,128]{4,3,2,1,0:T(8,128)S(1)} %get-tuple-element.19), channel_id=1, source_target_pairs={{0,1},{1,0},{2,3},{3,2},{4,5},{5,4},{6,7},{7,6},{8,9},{9,8},{10,11... | collective-permute-start | bytes 196616 | tf_op jit(solution)/shard_map/ppermute | solution.py:28
  6.0 11.1 %collective-permute-start.2 = (f32[2,4,16,128]{3,2,1,0:T(8,128)S(1)}, f32[2,4,16,128]{3,2,1,0:T(8,128)S(1)}, u32[]{:S(2)}, u32[]{:S(2)}) collective-permute-start(f32[2,4,16,128]{3,2,1,0:T(8,128)S(1)} %get-tuple-element.20), channel_id=1, source_target_pairs={{0,248},{1,251},{2,250},{3,253},{4,252},{5,255},{6,254},{7,1},{8,0... | collective-permute-start | bytes 196616 | tf_op jit(solution)/shard_map/ppermute | solution.py:24
  13.2 6.1 %collective-permute-start.4 = (f32[2,4,16,128]{3,2,1,0:T(8,128)S(1)}, f32[2,4,16,128]{3,2,1,0:T(8,128)S(1)}, u32[]{:S(2)}, u32[]{:S(2)}) collective-permute-start(f32[2,4,16,128]{3,2,1,0:T(8,128)S(1)} %get-tuple-element.22), channel_id=1, source_target_pairs={{0,254},{1,253},{2,0},{3,255},{4,2},{5,1},{6,4},{7,3},{8,6},{9,5},... | collective-permute-start | bytes 196616 | tf_op jit(solution)/shard_map/ppermute | solution.py:24
  19.2 6.8 %collective-permute-start.3 = (f32[4,128]{1,0:T(4,128)S(1)}, f32[4,128]{1,0:T(4,128)S(1)}, u32[]{:S(2)}, u32[]{:S(2)}) collective-permute-start(f32[4,128]{1,0:T(4,128)S(1)} %get-tuple-element.21), channel_id=1, source_target_pairs={{0,8},{1,7},{2,10},{3,9},{4,12},{5,11},{6,14},{7,13},{8,16},{9,15}... | collective-permute-start | bytes 6152 | tf_op jit(solution)/shard_map/ppermute | solution.py:24
  21.4 4.8 %collective-permute-start.8 = (f32[4,128]{1,0:T(4,128)S(1)}, f32[4,128]{1,0:T(4,128)S(1)}, u32[]{:S(2)}, u32[]{:S(2)}) collective-permute-start(f32[4,128]{1,0:T(4,128)S(1)} %get-tuple-element.25.own_ref), channel_id=1, source_target_pairs={{0,1},{1,0},{2,3},{3,2},{4,5},{5,4},{6,7},{7,6},{8,9},{9,8},{10,11... | collective-permute-start | bytes 6152 | tf_op jit(solution)/shard_map/ppermute | solution.py:28
  21.6 9.5 %collective-permute-start.5 = (f32[4,128]{1,0:T(4,128)S(1)}, f32[4,128]{1,0:T(4,128)S(1)}, u32[]{:S(2)}, u32[]{:S(2)}) collective-permute-start(f32[4,128]{1,0:T(4,128)S(1)} %get-tuple-element.24), channel_id=1, source_target_pairs={{0,2},{1,5},{2,4},{3,7},{4,6},{5,9},{6,8},{7,11},{8,10},{9,13},{10... | collective-permute-start | bytes 6152 | tf_op jit(solution)/shard_map/ppermute | solution.py:24
  24.0 8.4 %collective-permute-start.7 = (f32[4,128]{1,0:T(4,128)S(1)}, f32[4,128]{1,0:T(4,128)S(1)}, u32[]{:S(2)}, u32[]{:S(2)}) collective-permute-start(f32[4,128]{1,0:T(4,128)S(1)} %get-tuple-element.24), channel_id=1, source_target_pairs={{0,3},{1,4},{2,5},{3,6},{4,7},{5,8},{6,9},{7,10},{8,11},{9,12},{10... | collective-permute-start | bytes 6152 | tf_op jit(solution)/shard_map/ppermute | solution.py:24
  26.0 6.5 %collective-permute-start.6 = (f32[4,128]{1,0:T(4,128)S(1)}, f32[4,128]{1,0:T(4,128)S(1)}, u32[]{:S(2)}, u32[]{:S(2)}) collective-permute-start(f32[4,128]{1,0:T(4,128)S(1)} %collective-permute-done.3.refs_0_), channel_id=1, source_target_pairs={{0,1},{1,0},{2,3},{3,2},{4,5},{5,4},{6,7},{7,6},{8,9},{9,8},{10,11... | collective-permute-start | bytes 6152 | tf_op jit(solution)/shard_map/ppermute | solution.py:28
  26.2 6.3 %collective-permute-start.9 = (f32[2,128]{1,0:T(2,128)S(1)}, f32[2,128]{1,0:T(2,128)S(1)}, u32[]{:S(2)}, u32[]{:S(2)}) collective-permute-start(f32[2,128]{1,0:T(2,128)S(1)} %get-tuple-element.27), channel_id=1, source_target_pairs={{0,248},{1,249},{2,250},{3,251},{4,252},{5,253},{6,254},{7,255},{8... | collective-permute-start | bytes 3080 | tf_op jit(solution)/shard_map/ppermute | solution.py:24

commit v6 on v5

--- a/solution.py
+++ b/solution.py
@@ -49,7 +49,7 @@
 
 
 def step_of(m, rep):
-    return rep if m else 3 - rep
+    return 2 * rep if m else 3 - 2 * rep
 
 
 def pack_kernel(src_ref, active_ref, points_ref, normals_ref, index_ref, table_ref, *outs):
@@ -204,11 +204,7 @@
     back, totals = [], []
     for message, step in zip(there, steps):
         sums = pl.pallas_call(
-            near_kernel,
-            in_specs=[VMEM] * 2,
-            out_specs=VMEM,
-            out_shape=pltpu.VMEM((32, LANES), f32),
-            name="near",
+            near_kernel, in_specs=[VMEM] * 2, out_specs=VMEM, out_shape=pltpu.VMEM((32, LANES), f32), name="near"
         )(near(table), near(message))
         rows, last = pl.pallas_call(
             far_kernel,

time: 33.2 us -> 33.2 us (level)
  starting transfers between devices: 24.3 us -> 19.9 us
  waiting for transfers between devices: 2.35 us -> 6.73 us
    ppermute x7, waiting for transfers between devices: 1.45 us -> 5.82 us  [routed(): return lax.ppermute(block, ('blk', 'rep'), route)]
    ppermute x7, starting transfers between devices: 22.5 us -> 18.2 us  [routed(): return lax.ppermute(block, ('blk', 'rep'), route)]
  transfers between devices with their start and end apart: 10 -> 10, of which waited for: 2 -> 4; matrix products, arithmetic and copies ran while one was open for 0% -> 0% of each run, Pallas kernels for 12% -> 12%
where the time goes in v6:
time: 33.2 us; the launch traced here: 33.1 us
  starting transfers between devices  19.9 us (60%)
  waiting for transfers between devices  6.73 us (20%)
  Pallas kernels  5.78 us (17%)
  between operations  0.69 us (2%)
    ppermute x7, starting transfers between devices, routed(): return lax.ppermute(block, ('blk', 'rep'), route)  18.2 us
    ppermute x7, waiting for transfers between devices, routed(): return lax.ppermute(block, ('blk', 'rep'), route)  5.82 us
    pallas_call x2, Pallas kernels, body(): pl.pallas_call(far_kernel, in_specs=[VMEM] * (3 + len(totals)), out_specs...  2.12 us
    pallas_call x2, Pallas kernels, body(): pl.pallas_call(near_kernel, in_specs=[VMEM] * 2, out_specs=VMEM, out_shap...  1.95 us
    ppermute x3, starting transfers between devices, swapped(): return lax.ppermute(block, 'rep', [(0, 1), (1, 0)])  1.66 us
    pallas_call x1, Pallas kernels, body(): pl.pallas_call(pack_kernel, in_specs=[SMEM, SMEM, VMEM, VMEM, VMEM], out_...  1.08 us
    ppermute x3, waiting for transfers between devices, swapped(): return lax.ppermute(block, 'rep', [(0, 1), (1, 0)])  0.91 us
  transfers between devices with their start and end apart: 10, of which 4 were waited for; matrix products, arithmetic and copies ran while one was open for 0% of the time, Pallas kernels for 12%

profile of v6, /device:TPU:1, one launch (start us, length us, event | category | flops | bytes accessed | tf_op | source)
XLA Modules:
  0.0 33.1 jit_solution(5776702116451147476)
XLA Ops:
  0.6 1.1 %pack.1 = (f32[6,64,128]{2,1,0:T(8,128)S(1)}, f32[2,2,4,8,128]{4,3,2,1,0:T(8,128)S(1)}, f32[2,2,4,8,128]{4,3,2,1,0:T(8,128)S(1)}) custom-call(s32[8,8]{1,0:T(8,128)} %bitcast.11, s32[1,8]{1,0:T(1,128)} %bitcast.12, f32[3,64,128]{2,1,0:T(8,128)} %bitcast.8, f32[3,64,128]{2,1,0:T(8,128)} %bitcast.9, s32[8,8,128]{2,1,0:T(8,128)} %bitcast.10), custom_call_target="tpu_custom_call" | custom-call | tf_op jit(solution)/shard_map/pack/pallas_call | solution.py:179
  1.7 2.1 %collective-permute-start = (f32[6,64,128]{2,1,0:T(8,128)S(1)}, f32[6,64,128]{2,1,0:T(8,128)S(1)}, u32[]{:S(2)}, u32[]{:S(2)}) collective-permute-start(f32[6,64,128]{2,1,0:T(8,128)S(1)} %get-tuple-element.17.table_ref), channel_id=1, source_target_pairs={{0,8},{1,9},{2,10},{3,11},{4,12},{5,13},{6,14},{7,15},{8,16},{9,17... | collective-permute-start | bytes 589832 | tf_op jit(solution)/shard_map/ppermute | solution.py:24
  3.8 1.3 %collective-permute-start.1 = (f32[2,2,4,8,128]{4,3,2,1,0:T(8,128)S(1)}, f32[2,2,4,8,128]{4,3,2,1,0:T(8,128)S(1)}, u32[]{:S(2)}, u32[]{:S(2)}) collective-permute-start(f32[2,2,4,8,128]{4,3,2,1,0:T(8,128)S(1)} %get-tuple-element.19), channel_id=1, source_target_pairs={{0,1},{1,0},{2,3},{3,2},{4,5},{5,4},{6,7},{7,6},{8,9},{9,8},{10,11... | collective-permute-start | bytes 196616 | tf_op jit(solution)/shard_map/ppermute | solution.py:28
  5.1 0.9 %collective-permute-done.1.other_ref = f32[2,2,4,8,128]{4,3,2,1,0:T(8,128)S(1)} collective-permute-done((f32[2,2,4,8,128]{4,3,2,1,0:T(8,128)S(1)}, f32[2,2,4,8,128]{4,3,2,1,0:T(8,128)S(1)}, u32[]{:S(2)}, u32[]{:S(2)}) %collective-permute-start.1) | collective-permute-done | bytes 65568 | tf_op jit(solution)/shard_map/ppermute | solution.py:28
  6.0 8.8 %collective-permute-start.2 = (f32[2,4,16,128]{3,2,1,0:T(8,128)S(1)}, f32[2,4,16,128]{3,2,1,0:T(8,128)S(1)}, u32[]{:S(2)}, u32[]{:S(2)}) collective-permute-start(f32[2,4,16,128]{3,2,1,0:T(8,128)S(1)} %get-tuple-element.20), channel_id=1, source_target_pairs={{0,248},{1,253},{2,250},{3,255},{4,252},{5,1},{6,254},{7,3},{8,0},... | collective-permute-start | bytes 196616 | tf_op jit(solution)/shard_map/ppermute | solution.py:24
  14.8 1.8 %collective-permute-start.4 = (f32[2,4,16,128]{3,2,1,0:T(8,128)S(1)}, f32[2,4,16,128]{3,2,1,0:T(8,128)S(1)}, u32[]{:S(2)}, u32[]{:S(2)}) collective-permute-start(f32[2,4,16,128]{3,2,1,0:T(8,128)S(1)} %get-tuple-element.22), channel_id=1, source_target_pairs={{0,254},{1,251},{2,0},{3,253},{4,2},{5,255},{6,4},{7,1},{8,6},{9,3... | collective-permute-start | bytes 196616 | tf_op jit(solution)/shard_map/ppermute | solution.py:24
  16.5 0.0 collective-permute-done.2.message_ref
  16.5 1.0 %near.2.near_ref = f32[32,128]{1,0:T(8,128)S(1)} custom-call(f32[6,64,128]{2,1,0:T(8,128)S(1)} %get-tuple-element.17.table_ref, f32[2,4,16,128]{3,2,1,0:T(8,128)S(1)} %collective-permute-done.2.message_ref), custom_call_target="tpu_custom_call" | custom-call | tf_op jit(solution)/shard_map/near/pallas_call | solution.py:206
  17.5 0.0 collective-permute-done.table_ref
  17.5 1.1 %far.2 = (f32[4,128]{1,0:T(4,128)S(1)}, f32[4,128]{1,0:T(4,128)S(1)}) custom-call(f32[6,64,128]{2,1,0:T(8,128)S(1)} %collective-permute-done.table_ref, f32[2,4,16,128]{3,2,1,0:T(8,128)S(1)} %collective-permute-done.2.message_ref, f32[32,128]{1,0:T(8,128)S(1)} %near.2.near_ref), custom_call_target="tpu_custom_call" | custom-call | tf_op jit(solution)/shard_map/far/pallas_call | solution.py:209
  18.6 0.4 %collective-permute-start.3 = (f32[4,128]{1,0:T(4,128)S(1)}, f32[4,128]{1,0:T(4,128)S(1)}, u32[]{:S(2)}, u32[]{:S(2)}) collective-permute-start(f32[4,128]{1,0:T(4,128)S(1)} %get-tuple-element.21), channel_id=1, source_target_pairs={{0,8},{1,5},{2,10},{3,7},{4,12},{5,9},{6,14},{7,11},{8,16},{9,13},... | collective-permute-start | bytes 6152 | tf_op jit(solution)/shard_map/ppermute | solution.py:24
  19.0 0.1 collective-permute-done.4.message_ref
  19.1 1.0 %near.3.near_ref = f32[32,128]{1,0:T(8,128)S(1)} custom-call(f32[6,64,128]{2,1,0:T(8,128)S(1)} %get-tuple-element.17.table_ref, f32[2,4,16,128]{3,2,1,0:T(8,128)S(1)} %collective-permute-done.4.message_ref), custom_call_target="tpu_custom_call" | custom-call | tf_op jit(solution)/shard_map/near/pallas_call | solution.py:206
  20.1 1.1 %far.3 = (f32[4,128]{1,0:T(4,128)S(1)}, f32[4,128]{1,0:T(4,128)S(1)}) custom-call(f32[6,64,128]{2,1,0:T(8,128)S(1)} %collective-permute-done.table_ref, f32[2,4,16,128]{3,2,1,0:T(8,128)S(1)} %collective-permute-done.4.message_ref, f32[32,128]{1,0:T(8,128)S(1)} %near.3.near_ref, f32[4,128]{1,0:T(4,128)S(1)} %get-tuple-element.23.refs_0_), custom_call_target="tpu_custom_call" | custom-call | tf_op jit(solution)/shard_map/far/pallas_call | solution.py:209
  21.2 0.4 %collective-permute-start.8 = (f32[4,128]{1,0:T(4,128)S(1)}, f32[4,128]{1,0:T(4,128)S(1)}, u32[]{:S(2)}, u32[]{:S(2)}) collective-permute-start(f32[4,128]{1,0:T(4,128)S(1)} %get-tuple-element.25.own_ref), channel_id=1, source_target_pairs={{0,1},{1,0},{2,3},{3,2},{4,5},{5,4},{6,7},{7,6},{8,9},{9,8},{10,11... | collective-permute-start | bytes 6152 | tf_op jit(solution)/shard_map/ppermute | solution.py:28
  21.5 2.5 %collective-permute-start.5 = (f32[4,128]{1,0:T(4,128)S(1)}, f32[4,128]{1,0:T(4,128)S(1)}, u32[]{:S(2)}, u32[]{:S(2)}) collective-permute-start(f32[4,128]{1,0:T(4,128)S(1)} %get-tuple-element.24), channel_id=1, source_target_pairs={{0,2},{1,7},{2,4},{3,9},{4,6},{5,11},{6,8},{7,13},{8,10},{9,15},{1... | collective-permute-start | bytes 6152 | tf_op jit(solution)/shard_map/ppermute | solution.py:24
  24.0 0.1 collective-permute-start.7
  24.1 3.3 %collective-permute-done.3.refs_0_ = f32[4,128]{1,0:T(4,128)S(1)} collective-permute-done((f32[4,128]{1,0:T(4,128)S(1)}, f32[4,128]{1,0:T(4,128)S(1)}, u32[]{:S(2)}, u32[]{:S(2)}) %collective-permute-start.3) | collective-permute-done | bytes 2080 | tf_op jit(solution)/shard_map/ppermute | solution.py:24
  27.4 0.0 collective-permute-start.6
  27.4 0.0 collective-permute-done.8.other_ref
  27.4 2.6 %collective-permute-start.9 = (f32[2,128]{1,0:T(2,128)S(1)}, f32[2,128]{1,0:T(2,128)S(1)}, u32[]{:S(2)}, u32[]{:S(2)}) collective-permute-start(f32[2,128]{1,0:T(2,128)S(1)} %get-tuple-element.27), channel_id=1, source_target_pairs={{0,248},{1,249},{2,250},{3,251},{4,252},{5,253},{6,254},{7,255},{8... | collective-permute-start | bytes 3080 | tf_op jit(solution)/shard_map/ppermute | solution.py:24
  30.0 0.0 collective-permute-done.5.refs_1_
  30.0 2.5 %collective-permute-done.7.refs_3_ = f32[4,128]{1,0:T(4,128)S(1)} collective-permute-done((f32[4,128]{1,0:T(4,128)S(1)}, f32[4,128]{1,0:T(4,128)S(1)}, u32[]{:S(2)}, u32[]{:S(2)}) %collective-permute-start.7) | collective-permute-done | bytes 2080 | tf_op jit(solution)/shard_map/ppermute | solution.py:24
  32.5 0.0 collective-permute-done.9.refs_5_
  32.5 0.0 collective-permute-done.6.refs_2_
  32.5 0.6 %finish.1 = (f32[1,36]{1,0:T(1,128)}, f32[1,6]{1,0:T(1,128)}, f32[8,36]{1,0:T(8,128)}) custom-call(f32[4,128]{1,0:T(4,128)S(1)} %collective-permute-done.3.refs_0_, f32[4,128]{1,0:T(4,128)S(1)} %collective-permute-done.5.refs_1_, f32[4,128]{1,0:T(4,128)S(1)} %collective-permute-done.6.refs_2_, f32[4,128]{1,0:T(4,128)S(1)} %collective-permute-done.7.refs_3_, ...), custom_call_target="tpu_custom_call" | custom-call | tf_op jit(solution)/shard_map/finish/pallas_call | solution.py:230
  (2 shorter events, 0.0 us)
Async XLA Ops:
  1.7 15.8 %collective-permute-start = (f32[6,64,128]{2,1,0:T(8,128)S(1)}, f32[6,64,128]{2,1,0:T(8,128)S(1)}, u32[]{:S(2)}, u32[]{:S(2)}) collective-permute-start(f32[6,64,128]{2,1,0:T(8,128)S(1)} %get-tuple-element.17.table_ref), channel_id=1, source_target_pairs={{0,8},{1,9},{2,10},{3,11},{4,12},{5,13},{6,14},{7,15},{8,16},{9,17... | collective-permute-start | bytes 589832 | tf_op jit(solution)/shard_map/ppermute | solution.py:24
  3.8 2.2 %collective-permute-start.1 = (f32[2,2,4,8,128]{4,3,2,1,0:T(8,128)S(1)}, f32[2,2,4,8,128]{4,3,2,1,0:T(8,128)S(1)}, u32[]{:S(2)}, u32[]{:S(2)}) collective-permute-start(f32[2,2,4,8,128]{4,3,2,1,0:T(8,128)S(1)} %get-tuple-element.19), channel_id=1, source_target_pairs={{0,1},{1,0},{2,3},{3,2},{4,5},{5,4},{6,7},{7,6},{8,9},{9,8},{10,11... | collective-permute-start | bytes 196616 | tf_op jit(solution)/shard_map/ppermute | solution.py:28
  6.0 10.5 %collective-permute-start.2 = (f32[2,4,16,128]{3,2,1,0:T(8,128)S(1)}, f32[2,4,16,128]{3,2,1,0:T(8,128)S(1)}, u32[]{:S(2)}, u32[]{:S(2)}) collective-permute-start(f32[2,4,16,128]{3,2,1,0:T(8,128)S(1)} %get-tuple-element.20), channel_id=1, source_target_pairs={{0,248},{1,253},{2,250},{3,255},{4,252},{5,1},{6,254},{7,3},{8,0},... | collective-permute-start | bytes 196616 | tf_op jit(solution)/shard_map/ppermute | solution.py:24
  14.8 4.3 %collective-permute-start.4 = (f32[2,4,16,128]{3,2,1,0:T(8,128)S(1)}, f32[2,4,16,128]{3,2,1,0:T(8,128)S(1)}, u32[]{:S(2)}, u32[]{:S(2)}) collective-permute-start(f32[2,4,16,128]{3,2,1,0:T(8,128)S(1)} %get-tuple-element.22), channel_id=1, source_target_pairs={{0,254},{1,251},{2,0},{3,253},{4,2},{5,255},{6,4},{7,1},{8,6},{9,3... | collective-permute-start | bytes 196616 | tf_op jit(solution)/shard_map/ppermute | solution.py:24
  18.6 8.7 %collective-permute-start.3 = (f32[4,128]{1,0:T(4,128)S(1)}, f32[4,128]{1,0:T(4,128)S(1)}, u32[]{:S(2)}, u32[]{:S(2)}) collective-permute-start(f32[4,128]{1,0:T(4,128)S(1)} %get-tuple-element.21), channel_id=1, source_target_pairs={{0,8},{1,5},{2,10},{3,7},{4,12},{5,9},{6,14},{7,11},{8,16},{9,13},... | collective-permute-start | bytes 6152 | tf_op jit(solution)/shard_map/ppermute | solution.py:24
  21.2 6.2 %collective-permute-start.8 = (f32[4,128]{1,0:T(4,128)S(1)}, f32[4,128]{1,0:T(4,128)S(1)}, u32[]{:S(2)}, u32[]{:S(2)}) collective-permute-start(f32[4,128]{1,0:T(4,128)S(1)} %get-tuple-element.25.own_ref), channel_id=1, source_target_pairs={{0,1},{1,0},{2,3},{3,2},{4,5},{5,4},{6,7},{7,6},{8,9},{9,8},{10,11... | collective-permute-start | bytes 6152 | tf_op jit(solution)/shard_map/ppermute | solution.py:28
  21.5 8.4 %collective-permute-start.5 = (f32[4,128]{1,0:T(4,128)S(1)}, f32[4,128]{1,0:T(4,128)S(1)}, u32[]{:S(2)}, u32[]{:S(2)}) collective-permute-start(f32[4,128]{1,0:T(4,128)S(1)} %get-tuple-element.24), channel_id=1, source_target_pairs={{0,2},{1,7},{2,4},{3,9},{4,6},{5,11},{6,8},{7,13},{8,10},{9,15},{1... | collective-permute-start | bytes 6152 | tf_op jit(solution)/shard_map/ppermute | solution.py:24
  24.0 8.4 %collective-permute-start.7 = (f32[4,128]{1,0:T(4,128)S(1)}, f32[4,128]{1,0:T(4,128)S(1)}, u32[]{:S(2)}, u32[]{:S(2)}) collective-permute-start(f32[4,128]{1,0:T(4,128)S(1)} %get-tuple-element.24), channel_id=1, source_target_pairs={{0,3},{1,6},{2,5},{3,8},{4,7},{5,10},{6,9},{7,12},{8,11},{9,14},{1... | collective-permute-start | bytes 6152 | tf_op jit(solution)/shard_map/ppermute | solution.py:24
  27.4 5.1 %collective-permute-start.6 = (f32[4,128]{1,0:T(4,128)S(1)}, f32[4,128]{1,0:T(4,128)S(1)}, u32[]{:S(2)}, u32[]{:S(2)}) collective-permute-start(f32[4,128]{1,0:T(4,128)S(1)} %collective-permute-done.3.refs_0_), channel_id=1, source_target_pairs={{0,1},{1,0},{2,3},{3,2},{4,5},{5,4},{6,7},{7,6},{8,9},{9,8},{10,11... | collective-permute-start | bytes 6152 | tf_op jit(solution)/shard_map/ppermute | solution.py:28
  27.4 5.1 %collective-permute-start.9 = (f32[2,128]{1,0:T(2,128)S(1)}, f32[2,128]{1,0:T(2,128)S(1)}, u32[]{:S(2)}, u32[]{:S(2)}) collective-permute-start(f32[2,128]{1,0:T(2,128)S(1)} %get-tuple-element.27), channel_id=1, source_target_pairs={{0,248},{1,249},{2,250},{3,251},{4,252},{5,253},{6,254},{7,255},{8... | collective-permute-start | bytes 3080 | tf_op jit(solution)/shard_map/ppermute | solution.py:24
